TPU v7x, 256 devices: a whole 4x4x8 slice. The times are simulated.
256 devices in a mesh: side: 2 (over core), group: 16 (over y, z_lo), head: 8 (over x, z_hi).
Axes of the slice: x: 4, y: 4, z: 8 (z_hi: 2, z_lo: 4; z = z_hi * 4 + z_lo), core: 2. Of those that a mesh axis runs over, the one named last changes fastest.
Arguments:
- pool_rows: bfloat16 [2, 6144, 4096], P('side', ('group', 'head')), may hold values from -24 to 24
- pool_weight: bfloat16 [2, 4096, 8192], P('side', 'group', 'head'), as said below
- lengths: int32 [16, 3], replicated, may hold values from 1 to 192, 384 in all within a row
- owner: int32 [16, 3], replicated, may hold values from 0 to 15, as said below
Outputs:
- pool_out: bfloat16 [2, 6144, 4096], P('side', 'group', 'head')
Inputs may be any that keep to these rules, and one draw needn't show every extreme that they name: owner[p, j] is p with the binary digits of m_j flipped, where m_j = owner[0, j] is the same for every p; the m_j differ between slots, and every binary digit below 16 is set in some m_j. So the 3 requests of a prefill group go to different decode groups, and every decode group receives exactly one request for each slot j. `lengths`: each row sums to 384. `pool_weight`: independent normal entries of deviation 1 / sqrt(4096).
All inputs are finite; a program needn't handle non-finite values.
Results may differ from a plain program's by a relative error of at most 0.0061.
Values may be sent and summed in bfloat16 or wider, within the bound.
No kernel may reach another device: no remote copies, remote signals or barrier semaphores. Data moves between devices by JAX's collectives and lax.ppermute only.
A program may use at most 128 MiB of HBM per device.

v0:
```python
import jax
import jax.numpy as jnp
from jax import lax
from jax.experimental import pallas as pl
from jax.experimental.pallas import tpu as pltpu
from jax.sharding import Mesh
from jax.sharding import PartitionSpec as P


HEAD_DIM = 256
AXES = ("side", "y", "zl", "x", "zh")


def ring(value, axis, by):
    count = lax.axis_size(axis)
    return lax.ppermute(value, axis, [(i, (i + by) % count) for i in range(count)])


def ring_swap(value, bit):
    return lax.ppermute(value, "zl", [(i, i ^ bit) for i in range(4)])


def exchange(block, flip):
    groups = lax.axis_size("y") * lax.axis_size("zl")

    def route(by):
        pairs = [(p, groups + (p ^ by)) for p in range(groups)]
        return lambda b: lax.ppermute(b, ("side", "y", "zl"), pairs)

    return lax.switch(flip, [route(by) for by in range(groups)], block)


def turn(pos_ref, depth):
    y, zl = pos_ref[2], pos_ref[3]
    places = [y, (y + 3) & 3, (y + 1) & 3, (y + 2) & 3]
    return lambda k, d: pl.multiple_of((places[d] * 4 + (zl ^ k)) * depth, depth)


def blocks_of(refs):
    u, p, m, a, b = refs
    return [u[...], p[...], m[...], jnp.concatenate([a[...], b[...]], axis=0)]


def near_kernel(pos_ref, *refs):
    parts, near, (rows_ref, acc_ref) = refs[:8], refs[8:18], refs[18:]
    count = parts[0].shape[0]
    x, zh = pos_ref[0], pos_ref[1]
    places = [x, (x + 3) & 3, (x + 1) & 3, (x + 2) & 3]
    for i, part in enumerate(parts):
        which = zh if i < 4 else 1 - zh
        at = pl.multiple_of((2 * places[i % 4] + which) * count, 16)
        rows_ref[pl.ds(at, count), :] = part[...]
    at = turn(pos_ref, near[0].shape[0])
    for k in range(2):
        for d, block in enumerate(blocks_of(near[5 * k : 5 * k + 5])):
            cols = rows_ref[:, pl.ds(at(k, d), block.shape[0])]
            new = jnp.dot(cols, block, preferred_element_type=jnp.float32)
            if k == 0 and d == 0:
                acc_ref[...] = new
            else:
                acc_ref[...] += new


def far_kernel(pos_ref, rows_ref, sum_ref, *refs):
    far, (out_ref, acc_ref) = refs[:10], refs[10:]
    at = turn(pos_ref, far[0].shape[0])
    for k in range(2):
        for d, block in enumerate(blocks_of(far[5 * k : 5 * k + 5])):
            cols = rows_ref[:, pl.ds(at(k + 2, d), block.shape[0])]
            new = jnp.dot(cols, block, preferred_element_type=jnp.float32)
            if k == 0 and d == 0:
                acc_ref[...] = sum_ref[...] + new
            else:
                acc_ref[...] += new
    out_ref[...] = acc_ref[...].astype(jnp.bfloat16)


def spread_kernel(pos_ref, attended_ref, *refs):
    held, out_ref = refs[:20], refs[20]
    x, y, zl = pos_ref[0], pos_ref[2], pos_ref[3]
    wide = attended_ref.shape[1]
    steps = [(y - x) & 3, (y - x + 3) & 3, (y - x + 1) & 3, (y - x + 2) & 3]
    attended = attended_ref[...]
    for k in range(4):
        u, p, m, a, b = held[5 * k : 5 * k + 5]
        tails = [r[:, pl.ds(wide, wide)] for r in (u, p, m, a, b)]
        tails = tails[:3] + [jnp.concatenate(tails[3:], axis=0)]
        depth = u.shape[0]
        at = pl.multiple_of((zl ^ k) * depth, depth)
        for d in range(4):
            new = lax.dot_general(
                attended, tails[d], (((1,), (1,)), ((), ())), preferred_element_type=jnp.float32
            )
            out_ref[steps[d], :, pl.ds(at, depth)] = new.astype(jnp.bfloat16)


INSIDE = pl.BlockSpec(memory_space=pltpu.VMEM)


def inside_call(kernel, scalars, operands, outs, scratch=(), limit=40):
    many = isinstance(outs, (list, tuple))
    return pl.pallas_call(
        kernel,
        out_shape=outs,
        in_specs=[pl.BlockSpec(memory_space=pltpu.SMEM)] + [INSIDE] * len(operands),
        out_specs=[INSIDE] * len(outs) if many else INSIDE,
        scratch_shapes=list(scratch),
        compiler_params=pltpu.CompilerParams(vmem_limit_bytes=limit * 2**20),
    )(scalars, *operands)


def attend_kernel(lengths_ref, queries_ref, *refs):
    memories, out_ref = refs[:-1], refs[-1]
    wide = out_ref.shape[1]
    rows = out_ref.shape[0] // len(memories)
    scale = 1.0 / HEAD_DIM**0.5
    for j, memory_ref in enumerate(memories):
        mine = pl.ds(j * rows, rows)
        shape = (rows, memory_ref.shape[0])
        valid = lax.broadcasted_iota(jnp.int32, shape, 1) < lengths_ref[j]
        for e in range(wide // HEAD_DIM):
            cols = pl.ds(e * HEAD_DIM, HEAD_DIM)
            scores = lax.dot_general(
                queries_ref[mine, cols],
                memory_ref[:, cols],
                (((1,), (1,)), ((), ())),
                preferred_element_type=jnp.float32,
            )
            scores = jnp.where(valid, scores * scale, -1e30)
            peak = jnp.max(scores, axis=-1, keepdims=True)
            expo = jnp.where(valid, jnp.exp(scores - peak), 0.0)
            total = jnp.sum(expo, axis=-1, keepdims=True)
            values = memory_ref[:, pl.ds(wide + e * HEAD_DIM, HEAD_DIM)]
            mixed = jnp.dot(expo.astype(jnp.bfloat16), values, preferred_element_type=jnp.float32)
            out_ref[mine, cols] = (mixed / total).astype(jnp.bfloat16)


def attend(queries, memories, lengths):
    out = jax.ShapeDtypeStruct(queries.shape, jnp.bfloat16)
    return inside_call(attend_kernel, lengths, [queries, *memories], out, limit=12)


def body(pool_rows, pool_weight, lengths, owner):
    side = lax.axis_index("side")
    y, zl, x, zh = (lax.axis_index(a) for a in AXES[1:])
    requests = lengths.shape[1]
    w = pool_weight[0]
    mine = pool_rows[0]
    depth, width = w.shape
    wide = width // 2
    half = depth // 2
    count, model = mine.shape

    def both(value, axis):
        return ring(value, axis, 1), ring(value, axis, -1)

    def further(pair):
        return ring(pair[0][:half], "y", 1), ring(pair[1][half:], "y", -1)

    y0 = both(w, "y")
    u1 = ring_swap(w, 1)
    u2 = ring_swap(w, 2)
    x0 = both(mine, "x") + (ring(mine, "x", 2),)
    f0 = further(y0)
    y1 = both(u1, "y")
    u3 = ring_swap(u2, 1)
    other = lax.ppermute(mine, "zh", [(0, 1), (1, 0)])
    y2 = both(u2, "y")
    f1 = further(y1)
    y3 = both(u3, "y")
    f2 = further(y2)
    x1 = both(other, "x") + (ring(other, "x", 2),)
    f3 = further(y3)

    mem_g = 8 * count
    maxlen = mem_g // 2
    pos = jnp.stack([x, zh, y, zl]).astype(jnp.int32)
    held = [(w, *y0, *f0), (u1, *y1, *f1), (u2, *y2, *f2), (u3, *y3, *f3)]
    sums = jax.ShapeDtypeStruct((mem_g, width), jnp.float32)
    rows, acc = inside_call(
        near_kernel,
        pos,
        [mine, *x0, other, *x1, *held[0], *held[1]],
        [jax.ShapeDtypeStruct((mem_g, model), jnp.bfloat16), sums],
    )
    cached = inside_call(
        far_kernel,
        pos,
        [rows, acc, *held[2], *held[3]],
        jax.ShapeDtypeStruct((mem_g, width), jnp.bfloat16),
        scratch=[pltpu.VMEM((mem_g, width), jnp.float32)],
    )
    first = cached[:, :wide]

    group = y * 4 + zl
    flips = owner[0]
    own = lax.dynamic_index_in_dim(lengths, group, 0, keepdims=False)
    begins = jnp.cumsum(own) - own
    served = jnp.concatenate(
        [lax.dynamic_slice(lengths, (group ^ flips[j], j), (1, 1))[0] for j in range(requests)]
    )
    begins = [begins[j] for j in range(requests)]
    padded = jnp.concatenate([cached, jnp.zeros((maxlen, width), jnp.bfloat16)], axis=0)
    blocks = [lax.dynamic_slice(padded, (begins[j], 0), (maxlen, width)) for j in range(requests)]
    memories = [exchange(blocks[j], flips[j]) for j in range(requests)]
    attended = attend(first, memories, served)

    parts = inside_call(
        spread_kernel,
        pos,
        [attended, *held[0], *held[1], *held[2], *held[3]],
        jax.ShapeDtypeStruct((4, mem_g, width), jnp.bfloat16),
    )
    got = []
    for by in (2, 1, 3):
        pairs = [(4 + i, 4 + (i + by) % 4) for i in range(4)]
        got.append(lax.ppermute(parts[by], ("side", "x"), pairs))
    partial = parts[0].astype(jnp.float32)
    for g in got:
        partial = partial + g.astype(jnp.float32)
    low, high = partial[:, :wide], partial[:, wide:]
    give = jnp.where(zh == 0, high, low).astype(jnp.bfloat16)
    taken = lax.ppermute(give, ("side", "zh"), [(2, 3), (3, 2)])
    decoded = (jnp.where(zh == 0, low, high) + taken.astype(jnp.float32)).astype(jnp.bfloat16)
    return jnp.where(side == 0, first, decoded)[None]


def solution(mesh):
    torus = Mesh(mesh.devices.reshape(mesh.shape["side"], 4, 4, 4, 2), AXES)
    in_specs = (
        P("side", ("y", "zl", "x", "zh"), None),
        P("side", ("y", "zl"), ("x", "zh")),
        P(),
        P(),
    )
    out_specs = P("side", ("y", "zl"), ("x", "zh"))
    return jax.shard_map(body, mesh=torus, in_specs=in_specs, out_specs=out_specs, check_vma=False)
```

profile of v0, /device:TPU:17, one launch (start us, length us, event | category | flops | bytes accessed | tf_op | source)
XLA Modules:
  0.0 248.3 jit_solution(3619371816249779894)
XLA Ops:
  0.0 6.9 %collective-permute-start.51 = (bf16[48,4096]{1,0:T(8,128)(2,1)}, bf16[48,4096]{1,0:T(8,128)(2,1)}, u32[]{:S(2)}, u32[]{:S(2)}) collective-permute-start(bf16[48,4096]{1,0:T(8,128)(2,1)} %bitcast.37), channel_id=1, source_target_pairs={{0,1},{1,0},{2,3},{3,2},{4,5},{5,4},{6,7},{7,6},{8,9},{9,8},{10,11... | collective-permute-start | bytes 1179656 | tf_op jit(solution)/shard_map/ppermute | solution.py:167
  6.9 1.2 collective-permute-start.64
  9.8 1.2 collective-permute-start.48
  11.1 6.1 %collective-permute-done.51.refs_4_ = bf16[48,4096]{1,0:T(8,128)(2,1)} collective-permute-done((bf16[48,4096]{1,0:T(8,128)(2,1)}, bf16[48,4096]{1,0:T(8,128)(2,1)}, u32[]{:S(2)}, u32[]{:S(2)}) %collective-permute-start.51) | collective-permute-done | bytes 393248 | tf_op jit(solution)/shard_map/ppermute | solution.py:167
  17.2 2.5 collective-permute-start.49
  21.4 26.8 %collective-permute-done.64.refs_0_.refs_10_ = bf16[256,1024]{1,0:T(8,128)(2,1)S(1)} collective-permute-done((bf16[256,1024]{1,0:T(8,128)(2,1)}, bf16[256,1024]{1,0:T(8,128)(2,1)S(1)}, u32[]{:S(2)}, u32[]{:S(2)}) %collective-permute-start.64) | collective-permute-done | bytes 524320 | tf_op jit(solution)/shard_map/ppermute | solution.py:20
  49.2 2.7 %collective-permute-start.50 = (bf16[48,4096]{1,0:T(8,128)(2,1)}, bf16[48,4096]{1,0:T(8,128)(2,1)S(1)}, u32[]{:S(2)}, u32[]{:S(2)}) collective-permute-start(bf16[48,4096]{1,0:T(8,128)(2,1)} %bitcast.40), channel_id=1, source_target_pairs={{0,4},{2,6},{4,0},{6,2},{1,5},{3,7},{5,1},{7,3},{8,12},{10,14},{12... | collective-permute-start | bytes 1179656 | tf_op jit(solution)/shard_map/ppermute | solution.py:16
  52.8 7.8 %collective-permute-done.50.refs_3_ = bf16[48,4096]{1,0:T(8,128)(2,1)S(1)} collective-permute-done((bf16[48,4096]{1,0:T(8,128)(2,1)}, bf16[48,4096]{1,0:T(8,128)(2,1)S(1)}, u32[]{:S(2)}, u32[]{:S(2)}) %collective-permute-start.50) | collective-permute-done | bytes 393248 | tf_op jit(solution)/shard_map/ppermute | solution.py:16
  63.7 2.9 %collective-permute-done.57.refs_11_.refs_3_ = bf16[128,1024]{1,0:T(8,128)(2,1)S(1)} collective-permute-done((bf16[128,1024]{1,0:T(8,128)(2,1)S(1)}, bf16[128,1024]{1,0:T(8,128)(2,1)S(1)}, u32[]{:S(2)}, u32[]{:S(2)}) %collective-permute-start.57) | collective-permute-done | bytes 262176 | tf_op jit(solution)/shard_map/ppermute | solution.py:16
  68.3 1.3 collective-permute-start.70
  70.7 2.4 collective-permute-done.61.refs_15_.refs_7_
  73.2 1.2 collective-permute-start.52
  74.4 3.5 %collective-permute-done.65.refs_1_.refs_11_ = bf16[256,1024]{1,0:T(8,128)(2,1)S(1)} collective-permute-done((bf16[256,1024]{1,0:T(8,128)(2,1)S(1)}, bf16[256,1024]{1,0:T(8,128)(2,1)S(1)}, u32[]{:S(2)}, u32[]{:S(2)}) %collective-permute-start.65) | collective-permute-done | bytes 524320 | tf_op jit(solution)/shard_map/ppermute | solution.py:16
  77.9 2.5 collective-permute-start.53
  80.4 4.1 %collective-permute-done.66.refs_2_.refs_12_ = bf16[256,1024]{1,0:T(8,128)(2,1)S(1)} collective-permute-done((bf16[256,1024]{1,0:T(8,128)(2,1)S(1)}, bf16[256,1024]{1,0:T(8,128)(2,1)S(1)}, u32[]{:S(2)}, u32[]{:S(2)}) %collective-permute-start.66) | collective-permute-done | bytes 524320 | tf_op jit(solution)/shard_map/ppermute | solution.py:16
  84.5 2.7 %collective-permute-start.54 = (bf16[48,4096]{1,0:T(8,128)(2,1)}, bf16[48,4096]{1,0:T(8,128)(2,1)}, u32[]{:S(2)}, u32[]{:S(2)}) collective-permute-start(bf16[48,4096]{1,0:T(8,128)(2,1)} %collective-permute-done.51.refs_4_), channel_id=1, source_target_pairs={{0,4},{2,6},{4,0},{6,2},{1,5},{3,7},{5,1},{7,3},{8,12},{10,14},{12... | collective-permute-start | bytes 1179656 | tf_op jit(solution)/shard_map/ppermute | solution.py:16
  89.4 6.3 %collective-permute-done.71.refs_7_.refs_17_ = bf16[256,1024]{1,0:T(8,128)(2,1)S(1)} collective-permute-done((bf16[256,1024]{1,0:T(8,128)(2,1)S(1)}, bf16[256,1024]{1,0:T(8,128)(2,1)S(1)}, u32[]{:S(2)}, u32[]{:S(2)}) %collective-permute-start.71) | collective-permute-done | bytes 524320 | tf_op jit(solution)/shard_map/ppermute | solution.py:16
  95.7 1.6 collective-permute-start.62
  98.4 1.7 slice.97
  103.7 1.5 collective-permute-start.67
  105.2 1.5 collective-permute-start.72
  117.4 1.9 pad_add_fusion.1.lengths_ref
  121.5 1.0 copy-done.25
  122.5 1.0 copy-done.28
  129.4 3.6 %shard_map.46 = (bf16[384,4096]{1,0:T(8,128)(2,1)S(1)}, f32[384,1024]{1,0:T(8,128)S(1)}) custom-call(s32[4]{0:T(128)S(1)} %pad_add_fusion.pos_ref, bf16[48,4096]{1,0:T(8,128)(2,1)S(1)} %bitcast.41, bf16[48,4096]{1,0:T(8,128)(2,1)S(1)} %copy-done.38, bf16[48,4096]{1,0:T(8,128)(2,1)S(1)} %copy-done.40, bf16[48,4096]{1,0:T(8,128)(2,1)S(1)} %copy-done.42, ...), custom_call_target="tpu_custom_call" | custom-call | tf_op jit(solution)/shard_map/pallas_call | solution.py:102
  133.1 2.9 %shard_map.47 = bf16[384,1024]{1,0:T(8,128)(2,1)S(1)} custom-call(s32[4]{0:T(128)S(1)} %pad_add_fusion.pos_ref, bf16[384,4096]{1,0:T(8,128)(2,1)S(1)} %get-tuple-element.106.rows_ref, f32[384,1024]{1,0:T(8,128)S(1)} %get-tuple-element.107.sum_ref, bf16[256,1024]{1,0:T(8,128)(2,1)S(1)} %copy-done.20, ...), custom_call_target="tpu_custom_call" | custom-call | tf_op jit(solution)/shard_map/pallas_call | solution.py:102
  137.7 16.2 %conditional.3 = (bf16[192,1024]{1,0:T(8,128)(2,1)}) conditional(s32[]{:T(128)} %clamp.9, bf16[192,1024]{1,0:T(8,128)(2,1)S(1)} %get-tuple-element.113, bf16[192,1024]{1,0:T(8,128)(2,1)S(1)} %get-tuple-element.113, bf16[192,1024]{1,0:T(8,128)(2,1)S(1)} %get-tuple-element.113, ...), branch_computations={%region_1.2_spmd, %region_2.3_spmd, %region_3.4_spmd, %region_4.5_... | conditional | bytes 1572912 | solution.py:30
  137.7 1.3 collective-permute-start.15
  139.0 14.8 %collective-permute-done.15 = bf16[192,1024]{1,0:T(8,128)(2,1)} collective-permute-done((bf16[192,1024]{1,0:T(8,128)(2,1)S(1)}, bf16[192,1024]{1,0:T(8,128)(2,1)}, u32[]{:S(2)}, u32[]{:S(2)}) %collective-permute-start.15) | collective-permute-done | bytes 393248 | tf_op jit(solution)/shard_map/cond/branch_15_fun/ppermute | solution.py:28
  153.8 10.7 %conditional.4 = (bf16[192,1024]{1,0:T(8,128)(2,1)}) conditional(s32[]{:T(128)} %clamp.10, bf16[192,1024]{1,0:T(8,128)(2,1)S(1)} %get-tuple-element.112, bf16[192,1024]{1,0:T(8,128)(2,1)S(1)} %get-tuple-element.112, bf16[192,1024]{1,0:T(8,128)(2,1)S(1)} %get-tuple-element.112, ...), branch_computations={%region_17.18_spmd, %region_18.19_spmd, %region_19.20_spmd, %regio... | conditional | bytes 1572912 | solution.py:30
  153.8 1.3 collective-permute-start.24
  155.1 9.4 %collective-permute-done.24 = bf16[192,1024]{1,0:T(8,128)(2,1)} collective-permute-done((bf16[192,1024]{1,0:T(8,128)(2,1)S(1)}, bf16[192,1024]{1,0:T(8,128)(2,1)}, u32[]{:S(2)}, u32[]{:S(2)}) %collective-permute-start.24) | collective-permute-done | bytes 393248 | tf_op jit(solution)/shard_map/cond/branch_8_fun/ppermute | solution.py:28
  164.5 16.6 %conditional.5 = (bf16[192,1024]{1,0:T(8,128)(2,1)}) conditional(s32[]{:T(128)} %clamp.11, bf16[192,1024]{1,0:T(8,128)(2,1)S(1)} %get-tuple-element.111, bf16[192,1024]{1,0:T(8,128)(2,1)S(1)} %get-tuple-element.111, bf16[192,1024]{1,0:T(8,128)(2,1)S(1)} %get-tuple-element.111, ...), branch_computations={%region_33.34_spmd, %region_34.35_spmd, %region_35.36_spmd, %regio... | conditional | bytes 1572912 | solution.py:30
  164.5 1.3 collective-permute-start.46
  165.8 15.3 %collective-permute-done.46 = bf16[192,1024]{1,0:T(8,128)(2,1)} collective-permute-done((bf16[192,1024]{1,0:T(8,128)(2,1)S(1)}, bf16[192,1024]{1,0:T(8,128)(2,1)}, u32[]{:S(2)}, u32[]{:S(2)}) %collective-permute-start.46) | collective-permute-done | bytes 393248 | tf_op jit(solution)/shard_map/cond/branch_14_fun/ppermute | solution.py:28
  181.2 2.7 %shard_map.48.attended_ref = bf16[384,512]{1,0:T(8,128)(2,1)S(1)} custom-call(s32[3]{0:T(128)S(1)} %pad_add_fusion.1.lengths_ref, bf16[384,512]{1,0:T(8,128)(2,1)S(1)} %slice.102.queries_ref, bf16[192,1024]{1,0:T(8,128)(2,1)} %get-tuple-element.123.refs_0_, bf16[192,1024]{1,0:T(8,128)(2,1)} %get-tuple-element.124.refs_1_, ...), custom_call_target="tpu_custom_call" | custom-call | tf_op jit(solution)/shard_map/pallas_call | solution.py:102
  198.3 3.4 %shard_map.49 = bf16[4,384,1024]{2,1,0:T(8,128)(2,1)S(1)} custom-call(s32[4]{0:T(128)S(1)} %pad_add_fusion.pos_ref, bf16[384,512]{1,0:T(8,128)(2,1)S(1)} %shard_map.48.attended_ref, bf16[256,1024]{1,0:T(8,128)(2,1)S(1)} %bitcast.36, bf16[256,1024]{1,0:T(8,128)(2,1)S(1)} %copy-done.10, bf16[256,1024]{1,0:T(8,128)(2,1)S(1)} %copy-done.12, ...), custom_call_target="tpu_custom_call" | custom-call | tf_op jit(solution)/shard_map/pallas_call | solution.py:102
  201.7 1.5 slice_bitcast_fusion.2
  203.2 4.6 %collective-permute-start.74 = (bf16[384,1024]{1,0:T(8,128)(2,1)}, bf16[384,1024]{1,0:T(8,128)(2,1)}, u32[]{:S(2)}, u32[]{:S(2)}) collective-permute-start(bf16[384,1024]{1,0:T(8,128)(2,1)} %get-tuple-element.108), channel_id=1, source_target_pairs={{128,132},{130,134},{132,128},{134,130},{129,133},{131,135},{133,1... | collective-permute-start | bytes 2359304 | tf_op jit(solution)/shard_map/ppermute | solution.py:217
  207.8 2.2 collective-permute-start.75
  210.1 4.3 %collective-permute-start.76 = (bf16[384,1024]{1,0:T(8,128)(2,1)}, bf16[384,1024]{1,0:T(8,128)(2,1)}, u32[]{:S(2)}, u32[]{:S(2)}) collective-permute-start(bf16[384,1024]{1,0:T(8,128)(2,1)} %get-tuple-element.109), channel_id=1, source_target_pairs={{128,134},{130,128},{132,130},{134,132},{129,135},{131,129},{133,1... | collective-permute-start | bytes 2359304 | tf_op jit(solution)/shard_map/ppermute | solution.py:217
  214.4 3.5 %collective-permute-done.74 = bf16[384,1024]{1,0:T(8,128)(2,1)} collective-permute-done((bf16[384,1024]{1,0:T(8,128)(2,1)}, bf16[384,1024]{1,0:T(8,128)(2,1)}, u32[]{:S(2)}, u32[]{:S(2)}) %collective-permute-start.74) | collective-permute-done | bytes 786464 | tf_op jit(solution)/shard_map/ppermute | solution.py:217
  217.8 8.3 %collective-permute-done.75 = bf16[384,1024]{1,0:T(8,128)(2,1)} collective-permute-done((bf16[384,1024]{1,0:T(8,128)(2,1)}, bf16[384,1024]{1,0:T(8,128)(2,1)}, u32[]{:S(2)}, u32[]{:S(2)}) %collective-permute-start.75) | collective-permute-done | bytes 786464 | tf_op jit(solution)/shard_map/ppermute | solution.py:217
  226.3 3.3 %fusion.1 = f32[384,1024]{1,0:T(8,128)} fusion(bf16[384,1024]{1,0:T(8,128)(2,1)} %collective-permute-done.76, bf16[384,1024]{1,0:T(8,128)(2,1)} %collective-permute-done.75, bf16[384,1024]{1,0:T(8,128)(2,1)} %collective-permute-done.74, bf16[4,384,1024]{2,1,0:T(8,128)(2,1)S(1)} %shard_map.49), kind=kLoop, calls=%fused_computation.2 | loop fusion | flops 2752512 | bytes 4718592 | tf_op jit(solution)/shard_map/add | solution.py:220
  229.6 1.4 select_convert_fusion
  231.0 3.5 %collective-permute-start.77 = (bf16[384,512]{1,0:T(8,128)(2,1)S(1)}, bf16[384,512]{1,0:T(8,128)(2,1)S(1)}, u32[]{:S(2)}, u32[]{:S(2)}) collective-permute-start(bf16[384,512]{1,0:T(8,128)(2,1)S(1)} %select_convert_fusion), channel_id=1, source_target_pairs={{128,129},{129,128},{130,131},{131,130},{132,133},{133,132},{134,1... | collective-permute-start | bytes 1179656 | tf_op jit(solution)/shard_map/ppermute | solution.py:223
  234.6 11.3 %collective-permute-done.77 = bf16[384,512]{1,0:T(8,128)(2,1)S(1)} collective-permute-done((bf16[384,512]{1,0:T(8,128)(2,1)S(1)}, bf16[384,512]{1,0:T(8,128)(2,1)S(1)}, u32[]{:S(2)}, u32[]{:S(2)}) %collective-permute-start.77) | collective-permute-done | bytes 393248 | tf_op jit(solution)/shard_map/ppermute | solution.py:223
  245.8 2.5 fusion.3
  (137 shorter events, 43.5 us)
Async XLA Ops:
  0.0 97.4 %copy-start.44 = (s32[16,3]{0,1:T(4,128)S(1)}, s32[16,3]{0,1:T(4,128)}, u32[]{:S(2)}) copy-start(s32[16,3]{0,1:T(4,128)} %param.55) | copy-start | bytes 580
  0.0 98.0 %copy-start.43 = (s32[16,3]{0,1:T(4,128)S(1)}, s32[16,3]{0,1:T(4,128)}, u32[]{:S(2)}) copy-start(s32[16,3]{0,1:T(4,128)} %param.54) | copy-start | bytes 580
  0.0 17.2 %collective-permute-start.51 = (bf16[48,4096]{1,0:T(8,128)(2,1)}, bf16[48,4096]{1,0:T(8,128)(2,1)}, u32[]{:S(2)}, u32[]{:S(2)}) collective-permute-start(bf16[48,4096]{1,0:T(8,128)(2,1)} %bitcast.37), channel_id=1, source_target_pairs={{0,1},{1,0},{2,3},{3,2},{4,5},{5,4},{6,7},{7,6},{8,9},{9,8},{10,11... | collective-permute-start | bytes 1179656 | tf_op jit(solution)/shard_map/ppermute | solution.py:167
  6.9 41.3 %collective-permute-start.64 = (bf16[256,1024]{1,0:T(8,128)(2,1)}, bf16[256,1024]{1,0:T(8,128)(2,1)S(1)}, u32[]{:S(2)}, u32[]{:S(2)}) collective-permute-start(bf16[256,1024]{1,0:T(8,128)(2,1)} %bitcast.31), channel_id=1, source_target_pairs={{0,16},{8,24},{16,0},{24,8},{1,17},{9,25},{17,1},{25,9},{2,18},{10... | collective-permute-start | bytes 1572872 | tf_op jit(solution)/shard_map/ppermute | solution.py:20
  8.1 40.1 %collective-permute-start.59 = (bf16[256,1024]{1,0:T(8,128)(2,1)}, bf16[256,1024]{1,0:T(8,128)(2,1)S(1)}, u32[]{:S(2)}, u32[]{:S(2)}) collective-permute-start(bf16[256,1024]{1,0:T(8,128)(2,1)} %bitcast.32), channel_id=1, source_target_pairs={{0,8},{8,0},{16,24},{24,16},{1,9},{9,1},{17,25},{25,17},{2,10},{10... | collective-permute-start | bytes 1572872 | tf_op jit(solution)/shard_map/ppermute | solution.py:20
  8.8 40.4 %collective-permute-start.55 = (bf16[256,1024]{1,0:T(8,128)(2,1)}, bf16[256,1024]{1,0:T(8,128)(2,1)S(1)}, u32[]{:S(2)}, u32[]{:S(2)}) collective-permute-start(bf16[256,1024]{1,0:T(8,128)(2,1)} %bitcast.33), channel_id=1, source_target_pairs={{0,32},{32,64},{64,96},{96,0},{1,33},{33,65},{65,97},{97,1},{2,34}... | collective-permute-start | bytes 1572872 | tf_op jit(solution)/shard_map/ppermute | solution.py:16
  9.8 10.3 %collective-permute-start.48 = (bf16[48,4096]{1,0:T(8,128)(2,1)}, bf16[48,4096]{1,0:T(8,128)(2,1)S(1)}, u32[]{:S(2)}, u32[]{:S(2)}) collective-permute-start(bf16[48,4096]{1,0:T(8,128)(2,1)} %bitcast.38), channel_id=1, source_target_pairs={{0,2},{2,4},{4,6},{6,0},{1,3},{3,5},{5,7},{7,1},{8,10},{10,12},{12... | collective-permute-start | bytes 1179656 | tf_op jit(solution)/shard_map/ppermute | solution.py:16
  17.2 34.8 %collective-permute-start.49 = (bf16[48,4096]{1,0:T(8,128)(2,1)}, bf16[48,4096]{1,0:T(8,128)(2,1)S(1)}, u32[]{:S(2)}, u32[]{:S(2)}) collective-permute-start(bf16[48,4096]{1,0:T(8,128)(2,1)} %bitcast.39), channel_id=1, source_target_pairs={{0,6},{2,0},{4,2},{6,4},{1,7},{3,1},{5,3},{7,5},{8,14},{10,8},{12,... | collective-permute-start | bytes 1179656 | tf_op jit(solution)/shard_map/ppermute | solution.py:16
  20.9 41.8 %collective-permute-start.56 = (bf16[256,1024]{1,0:T(8,128)(2,1)}, bf16[256,1024]{1,0:T(8,128)(2,1)S(1)}, u32[]{:S(2)}, u32[]{:S(2)}) collective-permute-start(bf16[256,1024]{1,0:T(8,128)(2,1)} %bitcast.34), channel_id=1, source_target_pairs={{0,96},{32,0},{64,32},{96,64},{1,97},{33,1},{65,33},{97,65},{2,98}... | collective-permute-start | bytes 1572872 | tf_op jit(solution)/shard_map/ppermute | solution.py:16
  48.2 20.2 %collective-permute-start.69 = (bf16[256,1024]{1,0:T(8,128)(2,1)S(1)}, bf16[256,1024]{1,0:T(8,128)(2,1)S(1)}, u32[]{:S(2)}, u32[]{:S(2)}) collective-permute-start(bf16[256,1024]{1,0:T(8,128)(2,1)S(1)} %collective-permute-done.64.refs_0_.refs_10_), channel_id=1, source_target_pairs={{0,8},{8,0},{16,24},{24,16},{1,9},{9,1},{17,25},{25,17},{2,10},{10... | collective-permute-start | bytes 1572872 | tf_op jit(solution)/shard_map/ppermute | solution.py:20
  48.2 21.5 %collective-permute-start.60 = (bf16[256,1024]{1,0:T(8,128)(2,1)S(1)}, bf16[256,1024]{1,0:T(8,128)(2,1)S(1)}, u32[]{:S(2)}, u32[]{:S(2)}) collective-permute-start(bf16[256,1024]{1,0:T(8,128)(2,1)S(1)} %collective-permute-done.59.refs_13_.refs_5_), channel_id=1, source_target_pairs={{0,32},{32,64},{64,96},{96,0},{1,33},{33,65},{65,97},{97,1},{2,34}... | collective-permute-start | bytes 1572872 | tf_op jit(solution)/shard_map/ppermute | solution.py:16
  49.2 70.2 %copy-start.9 = (bf16[256,1024]{1,0:T(8,128)(2,1)}, bf16[256,1024]{1,0:T(8,128)(2,1)S(1)}, u32[]{:S(2)}) copy-start(bf16[256,1024]{1,0:T(8,128)(2,1)S(1)} %collective-permute-done.55.refs_9_.refs_1_) | copy-start | bytes 1572868
  49.2 11.5 %collective-permute-start.50 = (bf16[48,4096]{1,0:T(8,128)(2,1)}, bf16[48,4096]{1,0:T(8,128)(2,1)S(1)}, u32[]{:S(2)}, u32[]{:S(2)}) collective-permute-start(bf16[48,4096]{1,0:T(8,128)(2,1)} %bitcast.40), channel_id=1, source_target_pairs={{0,4},{2,6},{4,0},{6,2},{1,5},{3,7},{5,1},{7,3},{8,12},{10,14},{12... | collective-permute-start | bytes 1179656 | tf_op jit(solution)/shard_map/ppermute | solution.py:16
  52.7 13.9 %collective-permute-start.57 = (bf16[128,1024]{1,0:T(8,128)(2,1)S(1)}, bf16[128,1024]{1,0:T(8,128)(2,1)S(1)}, u32[]{:S(2)}, u32[]{:S(2)}) collective-permute-start(bf16[128,1024]{1,0:T(8,128)(2,1)S(1)} %slice.94), channel_id=1, source_target_pairs={{0,32},{32,64},{64,96},{96,0},{1,33},{33,65},{65,97},{97,1},{2,34}... | collective-permute-start | bytes 786440 | tf_op jit(solution)/shard_map/ppermute | solution.py:16
  61.5 11.7 %collective-permute-start.61 = (bf16[256,1024]{1,0:T(8,128)(2,1)S(1)}, bf16[256,1024]{1,0:T(8,128)(2,1)S(1)}, u32[]{:S(2)}, u32[]{:S(2)}) collective-permute-start(bf16[256,1024]{1,0:T(8,128)(2,1)S(1)} %collective-permute-done.59.refs_13_.refs_5_), channel_id=1, source_target_pairs={{0,96},{32,0},{64,32},{96,64},{1,97},{33,1},{65,33},{97,65},{2,98}... | collective-permute-start | bytes 1572872 | tf_op jit(solution)/shard_map/ppermute | solution.py:16
  62.7 56.7 %copy-start.11 = (bf16[256,1024]{1,0:T(8,128)(2,1)}, bf16[256,1024]{1,0:T(8,128)(2,1)S(1)}, u32[]{:S(2)}) copy-start(bf16[256,1024]{1,0:T(8,128)(2,1)S(1)} %collective-permute-done.56.refs_10_.refs_2_) | copy-start | bytes 1572868
  62.7 15.2 %collective-permute-start.65 = (bf16[256,1024]{1,0:T(8,128)(2,1)S(1)}, bf16[256,1024]{1,0:T(8,128)(2,1)S(1)}, u32[]{:S(2)}, u32[]{:S(2)}) collective-permute-start(bf16[256,1024]{1,0:T(8,128)(2,1)S(1)} %collective-permute-done.64.refs_0_.refs_10_), channel_id=1, source_target_pairs={{0,32},{32,64},{64,96},{96,0},{1,33},{33,65},{65,97},{97,1},{2,34}... | collective-permute-start | bytes 1572872 | tf_op jit(solution)/shard_map/ppermute | solution.py:16
  67.4 17.1 %collective-permute-start.66 = (bf16[256,1024]{1,0:T(8,128)(2,1)S(1)}, bf16[256,1024]{1,0:T(8,128)(2,1)S(1)}, u32[]{:S(2)}, u32[]{:S(2)}) collective-permute-start(bf16[256,1024]{1,0:T(8,128)(2,1)S(1)} %collective-permute-done.64.refs_0_.refs_10_), channel_id=1, source_target_pairs={{0,96},{32,0},{64,32},{96,64},{1,97},{33,1},{65,33},{97,65},{2,98}... | collective-permute-start | bytes 1572872 | tf_op jit(solution)/shard_map/ppermute | solution.py:16
  68.3 20.9 %collective-permute-start.70 = (bf16[256,1024]{1,0:T(8,128)(2,1)S(1)}, bf16[256,1024]{1,0:T(8,128)(2,1)S(1)}, u32[]{:S(2)}, u32[]{:S(2)}) collective-permute-start(bf16[256,1024]{1,0:T(8,128)(2,1)S(1)} %collective-permute-done.69.refs_5_.refs_15_), channel_id=1, source_target_pairs={{0,32},{32,64},{64,96},{96,0},{1,33},{33,65},{65,97},{97,1},{2,34}... | collective-permute-start | bytes 1572872 | tf_op jit(solution)/shard_map/ppermute | solution.py:16
  69.6 26.1 %copy-start.13 = (bf16[256,1024]{1,0:T(8,128)(2,1)}, bf16[256,1024]{1,0:T(8,128)(2,1)S(1)}, u32[]{:S(2)}) copy-start(bf16[256,1024]{1,0:T(8,128)(2,1)S(1)} %collective-permute-done.60.refs_14_.refs_6_) | copy-start | bytes 1572868
  69.7 26.1 %collective-permute-start.71 = (bf16[256,1024]{1,0:T(8,128)(2,1)S(1)}, bf16[256,1024]{1,0:T(8,128)(2,1)S(1)}, u32[]{:S(2)}, u32[]{:S(2)}) collective-permute-start(bf16[256,1024]{1,0:T(8,128)(2,1)S(1)} %collective-permute-done.69.refs_5_.refs_15_), channel_id=1, source_target_pairs={{0,96},{32,0},{64,32},{96,64},{1,97},{33,1},{65,33},{97,65},{2,98}... | collective-permute-start | bytes 1572872 | tf_op jit(solution)/shard_map/ppermute | solution.py:16
  73.2 11.3 %copy-start.16 = (bf16[256,1024]{1,0:T(8,128)(2,1)}, bf16[256,1024]{1,0:T(8,128)(2,1)S(1)}, u32[]{:S(2)}) copy-start(bf16[256,1024]{1,0:T(8,128)(2,1)S(1)} %collective-permute-done.61.refs_15_.refs_7_) | copy-start | bytes 1572868
  73.2 30.5 %collective-permute-start.52 = (bf16[48,4096]{1,0:T(8,128)(2,1)}, bf16[48,4096]{1,0:T(8,128)(2,1)}, u32[]{:S(2)}, u32[]{:S(2)}) collective-permute-start(bf16[48,4096]{1,0:T(8,128)(2,1)} %collective-permute-done.51.refs_4_), channel_id=1, source_target_pairs={{0,2},{2,4},{4,6},{6,0},{1,3},{3,5},{5,7},{7,1},{8,10},{10,12},{12... | collective-permute-start | bytes 1179656 | tf_op jit(solution)/shard_map/ppermute | solution.py:16
  77.9 55.2 %copy-start.1 = (bf16[256,1024]{1,0:T(8,128)(2,1)}, bf16[256,1024]{1,0:T(8,128)(2,1)S(1)}, u32[]{:S(2)}) copy-start(bf16[256,1024]{1,0:T(8,128)(2,1)S(1)} %collective-permute-done.65.refs_1_.refs_11_) | copy-start | bytes 1572868
  77.9 27.3 %collective-permute-start.53 = (bf16[48,4096]{1,0:T(8,128)(2,1)}, bf16[48,4096]{1,0:T(8,128)(2,1)}, u32[]{:S(2)}, u32[]{:S(2)}) collective-permute-start(bf16[48,4096]{1,0:T(8,128)(2,1)} %collective-permute-done.51.refs_4_), channel_id=1, source_target_pairs={{0,6},{2,0},{4,2},{6,4},{1,7},{3,1},{5,3},{7,5},{8,14},{10,8},{12,... | collective-permute-start | bytes 1179656 | tf_op jit(solution)/shard_map/ppermute | solution.py:16
  84.5 48.6 %copy-start.3 = (bf16[256,1024]{1,0:T(8,128)(2,1)}, bf16[256,1024]{1,0:T(8,128)(2,1)S(1)}, u32[]{:S(2)}) copy-start(bf16[256,1024]{1,0:T(8,128)(2,1)S(1)} %collective-permute-done.66.refs_2_.refs_12_) | copy-start | bytes 1572868
  84.5 20.6 %collective-permute-start.54 = (bf16[48,4096]{1,0:T(8,128)(2,1)}, bf16[48,4096]{1,0:T(8,128)(2,1)}, u32[]{:S(2)}, u32[]{:S(2)}) collective-permute-start(bf16[48,4096]{1,0:T(8,128)(2,1)} %collective-permute-done.51.refs_4_), channel_id=1, source_target_pairs={{0,4},{2,6},{4,0},{6,2},{1,5},{3,7},{5,1},{7,3},{8,12},{10,14},{12... | collective-permute-start | bytes 1179656 | tf_op jit(solution)/shard_map/ppermute | solution.py:16
  89.2 43.8 %copy-start.5 = (bf16[256,1024]{1,0:T(8,128)(2,1)}, bf16[256,1024]{1,0:T(8,128)(2,1)S(1)}, u32[]{:S(2)}) copy-start(bf16[256,1024]{1,0:T(8,128)(2,1)S(1)} %collective-permute-done.70.refs_6_.refs_16_) | copy-start | bytes 1572868
  89.2 13.7 %collective-permute-start.58 = (bf16[128,1024]{1,0:T(8,128)(2,1)}, bf16[128,1024]{1,0:T(8,128)(2,1)S(1)}, u32[]{:S(2)}, u32[]{:S(2)}) collective-permute-start(bf16[128,1024]{1,0:T(8,128)(2,1)} %slice.95), channel_id=1, source_target_pairs={{0,96},{32,0},{64,32},{96,64},{1,97},{33,1},{65,33},{97,65},{2,98}... | collective-permute-start | bytes 786440 | tf_op jit(solution)/shard_map/ppermute | solution.py:16
  95.7 37.3 %copy-start.7 = (bf16[256,1024]{1,0:T(8,128)(2,1)}, bf16[256,1024]{1,0:T(8,128)(2,1)S(1)}, u32[]{:S(2)}) copy-start(bf16[256,1024]{1,0:T(8,128)(2,1)S(1)} %collective-permute-done.71.refs_7_.refs_17_) | copy-start | bytes 1572868
  95.7 10.9 %collective-permute-start.62 = (bf16[128,1024]{1,0:T(8,128)(2,1)}, bf16[128,1024]{1,0:T(8,128)(2,1)}, u32[]{:S(2)}, u32[]{:S(2)}) collective-permute-start(bf16[128,1024]{1,0:T(8,128)(2,1)} %slice.96), channel_id=1, source_target_pairs={{0,32},{32,64},{64,96},{96,0},{1,33},{33,65},{65,97},{97,1},{2,34}... | collective-permute-start | bytes 786440 | tf_op jit(solution)/shard_map/ppermute | solution.py:16
  103.7 15.7 %collective-permute-start.63 = (bf16[128,1024]{1,0:T(8,128)(2,1)}, bf16[128,1024]{1,0:T(8,128)(2,1)}, u32[]{:S(2)}, u32[]{:S(2)}) collective-permute-start(bf16[128,1024]{1,0:T(8,128)(2,1)} %slice.97), channel_id=1, source_target_pairs={{0,96},{32,0},{64,32},{96,64},{1,97},{33,1},{65,33},{97,65},{2,98}... | collective-permute-start | bytes 786440 | tf_op jit(solution)/shard_map/ppermute | solution.py:16
  103.7 29.3 %collective-permute-start.67 = (bf16[128,1024]{1,0:T(8,128)(2,1)}, bf16[128,1024]{1,0:T(8,128)(2,1)S(1)}, u32[]{:S(2)}, u32[]{:S(2)}) collective-permute-start(bf16[128,1024]{1,0:T(8,128)(2,1)} %slice.98), channel_id=1, source_target_pairs={{0,32},{32,64},{64,96},{96,0},{1,33},{33,65},{65,97},{97,1},{2,34}... | collective-permute-start | bytes 786440 | tf_op jit(solution)/shard_map/ppermute | solution.py:16
  105.2 27.9 %collective-permute-start.68 = (bf16[128,1024]{1,0:T(8,128)(2,1)}, bf16[128,1024]{1,0:T(8,128)(2,1)}, u32[]{:S(2)}, u32[]{:S(2)}) collective-permute-start(bf16[128,1024]{1,0:T(8,128)(2,1)} %slice.99), channel_id=1, source_target_pairs={{0,96},{32,0},{64,32},{96,64},{1,97},{33,1},{65,33},{97,65},{2,98}... | collective-permute-start | bytes 786440 | tf_op jit(solution)/shard_map/ppermute | solution.py:16
  105.2 27.9 %collective-permute-start.72 = (bf16[128,1024]{1,0:T(8,128)(2,1)}, bf16[128,1024]{1,0:T(8,128)(2,1)}, u32[]{:S(2)}, u32[]{:S(2)}) collective-permute-start(bf16[128,1024]{1,0:T(8,128)(2,1)} %slice.100), channel_id=1, source_target_pairs={{0,32},{32,64},{64,96},{96,0},{1,33},{33,65},{65,97},{97,1},{2,34}... | collective-permute-start | bytes 786440 | tf_op jit(solution)/shard_map/ppermute | solution.py:16
  106.6 26.4 %collective-permute-start.73 = (bf16[128,1024]{1,0:T(8,128)(2,1)}, bf16[128,1024]{1,0:T(8,128)(2,1)}, u32[]{:S(2)}, u32[]{:S(2)}) collective-permute-start(bf16[128,1024]{1,0:T(8,128)(2,1)} %slice.101), channel_id=1, source_target_pairs={{0,96},{32,0},{64,32},{96,64},{1,97},{33,1},{65,33},{97,65},{2,98}... | collective-permute-start | bytes 786440 | tf_op jit(solution)/shard_map/ppermute | solution.py:16
  119.4 1.0 copy-start.14
  120.4 1.0 copy-start.17
  129.4 3.7 %copy-start.20 = (bf16[256,1024]{1,0:T(8,128)(2,1)S(1)}, bf16[256,1024]{1,0:T(8,128)(2,1)}, u32[]{:S(2)}) copy-start(bf16[256,1024]{1,0:T(8,128)(2,1)} %copy-done.19) | copy-start | bytes 1572868
  129.4 3.7 %copy-start.23 = (bf16[256,1024]{1,0:T(8,128)(2,1)S(1)}, bf16[256,1024]{1,0:T(8,128)(2,1)}, u32[]{:S(2)}) copy-start(bf16[256,1024]{1,0:T(8,128)(2,1)} %copy-done.22) | copy-start | bytes 1572868
  137.7 16.1 %collective-permute-start.15 = (bf16[192,1024]{1,0:T(8,128)(2,1)S(1)}, bf16[192,1024]{1,0:T(8,128)(2,1)}, u32[]{:S(2)}, u32[]{:S(2)}) collective-permute-start(bf16[192,1024]{1,0:T(8,128)(2,1)S(1)} %param.15), channel_id=1, source_target_pairs={{0,248},{8,240},{16,232},{24,224},{32,216},{40,208},{48,200},{56,1... | collective-permute-start | bytes 1179656 | tf_op jit(solution)/shard_map/cond/branch_15_fun/ppermute | solution.py:28
  153.8 10.7 %collective-permute-start.24 = (bf16[192,1024]{1,0:T(8,128)(2,1)S(1)}, bf16[192,1024]{1,0:T(8,128)(2,1)}, u32[]{:S(2)}, u32[]{:S(2)}) collective-permute-start(bf16[192,1024]{1,0:T(8,128)(2,1)S(1)} %param.24), channel_id=1, source_target_pairs={{0,192},{8,200},{16,208},{24,216},{32,224},{40,232},{48,240},{56,2... | collective-permute-start | bytes 1179656 | tf_op jit(solution)/shard_map/cond/branch_8_fun/ppermute | solution.py:28
  164.5 16.6 %collective-permute-start.46 = (bf16[192,1024]{1,0:T(8,128)(2,1)S(1)}, bf16[192,1024]{1,0:T(8,128)(2,1)}, u32[]{:S(2)}, u32[]{:S(2)}) collective-permute-start(bf16[192,1024]{1,0:T(8,128)(2,1)S(1)} %param.46), channel_id=1, source_target_pairs={{0,240},{8,248},{16,224},{24,232},{32,208},{40,216},{48,192},{56,2... | collective-permute-start | bytes 1179656 | tf_op jit(solution)/shard_map/cond/branch_14_fun/ppermute | solution.py:28
  183.9 1.0 copy-start.2
  203.2 14.6 %collective-permute-start.74 = (bf16[384,1024]{1,0:T(8,128)(2,1)}, bf16[384,1024]{1,0:T(8,128)(2,1)}, u32[]{:S(2)}, u32[]{:S(2)}) collective-permute-start(bf16[384,1024]{1,0:T(8,128)(2,1)} %get-tuple-element.108), channel_id=1, source_target_pairs={{128,132},{130,134},{132,128},{134,130},{129,133},{131,135},{133,1... | collective-permute-start | bytes 2359304 | tf_op jit(solution)/shard_map/ppermute | solution.py:217
  207.8 18.3 %collective-permute-start.75 = (bf16[384,1024]{1,0:T(8,128)(2,1)}, bf16[384,1024]{1,0:T(8,128)(2,1)}, u32[]{:S(2)}, u32[]{:S(2)}) collective-permute-start(bf16[384,1024]{1,0:T(8,128)(2,1)} %get-tuple-element.110), channel_id=1, source_target_pairs={{128,130},{130,132},{132,134},{134,128},{129,131},{131,133},{133,1... | collective-permute-start | bytes 2359304 | tf_op jit(solution)/shard_map/ppermute | solution.py:217
  210.1 16.2 %collective-permute-start.76 = (bf16[384,1024]{1,0:T(8,128)(2,1)}, bf16[384,1024]{1,0:T(8,128)(2,1)}, u32[]{:S(2)}, u32[]{:S(2)}) collective-permute-start(bf16[384,1024]{1,0:T(8,128)(2,1)} %get-tuple-element.109), channel_id=1, source_target_pairs={{128,134},{130,128},{132,130},{134,132},{129,135},{131,129},{133,1... | collective-permute-start | bytes 2359304 | tf_op jit(solution)/shard_map/ppermute | solution.py:217
  231.0 14.8 %collective-permute-start.77 = (bf16[384,512]{1,0:T(8,128)(2,1)S(1)}, bf16[384,512]{1,0:T(8,128)(2,1)S(1)}, u32[]{:S(2)}, u32[]{:S(2)}) collective-permute-start(bf16[384,512]{1,0:T(8,128)(2,1)S(1)} %select_convert_fusion), channel_id=1, source_target_pairs={{128,129},{129,128},{130,131},{131,130},{132,133},{133,132},{134,1... | collective-permute-start | bytes 1179656 | tf_op jit(solution)/shard_map/ppermute | solution.py:223
  (30 other events, 28.3 us)
where the time goes:
time: 250 us; the launch traced here: 248 us
  waiting for transfers between devices  124 us (50%)
  starting transfers between devices  50.9 us (20%)
  local copies, waits for them, and re-layouts  41.8 us (17%)
  Pallas kernels  12.6 us (5%)
  between operations  9.61 us (4%)
  other arithmetic  9.4 us (4%)
    ppermute x3, waiting for transfers between devices, route(): return lambda b: lax.ppermute(b, ('side', 'y', 'zl'), pairs)  39.6 us
    unnamed x90, local copies, waits for them, and re-layouts  31.4 us
    ppermute x22, waiting for transfers between devices, ring(): lax.ppermute(value, axis, [(i, (i + by) % count) for i in range(count)])  28.3 us
    ppermute x3, waiting for transfers between devices, ring_swap(): return lax.ppermute(value, 'zl', [(i, i ^ bit) for i in range(4)])  26.8 us
    ppermute x22, starting transfers between devices, ring(): lax.ppermute(value, axis, [(i, (i + by) % count) for i in range(count)])  23.5 us
    pallas_call x4, Pallas kernels, inside_call(): pl.pallas_call(kernel, out_shape=outs, in_specs=[pl.BlockSpec(memory_spac...  12.6 us
    ppermute x3, waiting for transfers between devices, body(): got.append(lax.ppermute(parts[by], ('side', 'x'), pairs))  11.9 us
    ppermute x1, waiting for transfers between devices, body(): taken = lax.ppermute(give, ('side', 'zh'), [(2, 3), (3, 2)])  11.3 us
  transfers between devices with their start and end apart: 33, of which 17 were waited for; matrix products, arithmetic and copies ran while one was open for 4% of the time, Pallas kernels for 1%

commit v1 on v0

--- a/solution.py
+++ b/solution.py
@@ -36,77 +36,127 @@
     return lambda k, d: pl.multiple_of((places[d] * 4 + (zl ^ k)) * depth, depth)
 
 
-def blocks_of(refs):
-    u, p, m, a, b = refs
-    return [u[...], p[...], m[...], jnp.concatenate([a[...], b[...]], axis=0)]
+def fetch(held, buf_ref, sems):
+    copies = []
+    for k in range(2):
+        u, p, m, a, b = held[5 * k : 5 * k + 5]
+        half = a.shape[0]
+        spots = [buf_ref.at[k, d] for d in range(3)]
+        spots += [buf_ref.at[k, 3, pl.ds(0, half)], buf_ref.at[k, 3, pl.ds(half, half)]]
+        for i, (src, dst) in enumerate(zip((u, p, m, a, b), spots)):
+            copies.append(pltpu.make_async_copy(src, dst, sems.at[5 * k + i]))
+    return copies
+
+
+def accumulate(rows_ref, acc_ref, buf_ref, copies, at, base):
+    depth = buf_ref.shape[2]
+    for k in range(2):
+        for d in range(4):
+            for copy in copies[5 * k + d : 5 * k + d + (2 if d == 3 else 1)]:
+                copy.wait()
+            cols = rows_ref[:, pl.ds(at(k + base, d), depth)]
+            new = jnp.dot(cols, buf_ref[k, d], preferred_element_type=jnp.float32)
+            if base == 0 and k == 0 and d == 0:
+                acc_ref[...] = new
+            else:
+                acc_ref[...] += new
 
 
 def near_kernel(pos_ref, *refs):
-    parts, near, (rows_ref, acc_ref) = refs[:8], refs[8:18], refs[18:]
+    parts, near, (rows_ref, acc_ref, buf_ref, row_sems, sems) = refs[:8], refs[8:18], refs[18:]
     count = parts[0].shape[0]
     x, zh = pos_ref[0], pos_ref[1]
     places = [x, (x + 3) & 3, (x + 1) & 3, (x + 2) & 3]
+    fills = []
     for i, part in enumerate(parts):
         which = zh if i < 4 else 1 - zh
         at = pl.multiple_of((2 * places[i % 4] + which) * count, 16)
-        rows_ref[pl.ds(at, count), :] = part[...]
-    at = turn(pos_ref, near[0].shape[0])
-    for k in range(2):
-        for d, block in enumerate(blocks_of(near[5 * k : 5 * k + 5])):
-            cols = rows_ref[:, pl.ds(at(k, d), block.shape[0])]
-            new = jnp.dot(cols, block, preferred_element_type=jnp.float32)
-            if k == 0 and d == 0:
-                acc_ref[...] = new
-            else:
-                acc_ref[...] += new
+        fills.append(pltpu.make_async_copy(part, rows_ref.at[pl.ds(at, count)], row_sems.at[i]))
+    copies = fetch(near, buf_ref, sems)
+    for copy in fills + copies:
+        copy.start()
+    for copy in fills:
+        copy.wait()
+    accumulate(rows_ref, acc_ref, buf_ref, copies, turn(pos_ref, buf_ref.shape[2]), 0)
 
 
 def far_kernel(pos_ref, rows_ref, sum_ref, *refs):
-    far, (out_ref, acc_ref) = refs[:10], refs[10:]
-    at = turn(pos_ref, far[0].shape[0])
-    for k in range(2):
-        for d, block in enumerate(blocks_of(far[5 * k : 5 * k + 5])):
-            cols = rows_ref[:, pl.ds(at(k + 2, d), block.shape[0])]
-            new = jnp.dot(cols, block, preferred_element_type=jnp.float32)
-            if k == 0 and d == 0:
-                acc_ref[...] = sum_ref[...] + new
-            else:
-                acc_ref[...] += new
+    far, (out_ref, acc_ref, buf_ref, sems) = refs[:10], refs[10:]
+    copies = fetch(far, buf_ref, sems)
+    for copy in copies:
+        copy.start()
+    acc_ref[...] = sum_ref[...]
+    accumulate(rows_ref, acc_ref, buf_ref, copies, turn(pos_ref, buf_ref.shape[2]), 2)
     out_ref[...] = acc_ref[...].astype(jnp.bfloat16)
 
 
 def spread_kernel(pos_ref, attended_ref, *refs):
-    held, out_ref = refs[:20], refs[20]
+    held, outs, (buf_ref, sems) = refs[:20], refs[20:24], refs[24:]
     x, y, zl = pos_ref[0], pos_ref[2], pos_ref[3]
     wide = attended_ref.shape[1]
     steps = [(y - x) & 3, (y - x + 3) & 3, (y - x + 1) & 3, (y - x + 2) & 3]
+    depth = held[0].shape[0]
+    half = depth // 2
+    tail = pl.ds(wide, wide)
+
+    def start(src, i, at, rows):
+        dst = buf_ref.at[i, pl.ds(at, rows)]
+        pltpu.make_async_copy(src.at[:, tail], dst, sems.at[i]).start()
+
+    for i, by in enumerate((2, 1, 3, 0)):
+        for d in range(4):
+
+            @pl.when(steps[d] == by)
+            def _():
+                for k in range(4):
+                    at = pl.multiple_of((zl ^ k) * depth, depth)
+                    if d < 3:
+                        start(held[5 * k + d], i, at, depth)
+                    else:
+                        start(held[5 * k + 3], i, at, half)
+                        start(held[5 * k + 4], i, pl.multiple_of(at + half, half), half)
+
     attended = attended_ref[...]
-    for k in range(4):
-        u, p, m, a, b = held[5 * k : 5 * k + 5]
-        tails = [r[:, pl.ds(wide, wide)] for r in (u, p, m, a, b)]
-        tails = tails[:3] + [jnp.concatenate(tails[3:], axis=0)]
-        depth = u.shape[0]
-        at = pl.multiple_of((zl ^ k) * depth, depth)
-        for d in range(4):
-            new = lax.dot_general(
-                attended, tails[d], (((1,), (1,)), ((), ())), preferred_element_type=jnp.float32
-            )
-            out_ref[steps[d], :, pl.ds(at, depth)] = new.astype(jnp.bfloat16)
+    for i, out_ref in enumerate(outs):
+        pltpu.make_async_copy(buf_ref.at[i], buf_ref.at[i], sems.at[i]).wait()
+        new = lax.dot_general(
+            attended, buf_ref[i], (((1,), (1,)), ((), ())), preferred_element_type=jnp.float32
+        )
+        out_ref[...] = new.astype(out_ref.dtype)
+
+
+def collect_kernel(pos_ref, own_ref, *refs):
+    got, (keep_ref, give_ref, buf_ref, sems) = refs[:3], refs[3:]
+    copies = [pltpu.make_async_copy(g, buf_ref.at[i], sems.at[i]) for i, g in enumerate(got)]
+    for copy in copies:
+        copy.start()
+    total = own_ref[...]
+    for i, copy in enumerate(copies):
+        copy.wait()
+        total = total + buf_ref[i].astype(jnp.float32)
+    wide = keep_ref.shape[1]
+    low, high = total[:, :wide], total[:, wide:]
+    mine = pos_ref[1] == 0
+    keep_ref[...] = jnp.where(mine, low, high)
+    give_ref[...] = jnp.where(mine, high, low).astype(jnp.bfloat16)
 
 
 INSIDE = pl.BlockSpec(memory_space=pltpu.VMEM)
-
-
-def inside_call(kernel, scalars, operands, outs, scratch=(), limit=40):
+ANYWHERE = pl.BlockSpec(memory_space=pltpu.HBM)
+
+
+def call(kernel, scalars, inside, anywhere, outs, scratch=(), limit=40):
     many = isinstance(outs, (list, tuple))
     return pl.pallas_call(
         kernel,
         out_shape=outs,
-        in_specs=[pl.BlockSpec(memory_space=pltpu.SMEM)] + [INSIDE] * len(operands),
+        in_specs=[pl.BlockSpec(memory_space=pltpu.SMEM)]
+        + [INSIDE] * len(inside)
+        + [ANYWHERE] * len(anywhere),
         out_specs=[INSIDE] * len(outs) if many else INSIDE,
         scratch_shapes=list(scratch),
         compiler_params=pltpu.CompilerParams(vmem_limit_bytes=limit * 2**20),
-    )(scalars, *operands)
+    )(scalars, *inside, *anywhere)
 
 
 def attend_kernel(lengths_ref, queries_ref, *refs):
@@ -137,7 +187,7 @@
 
 def attend(queries, memories, lengths):
     out = jax.ShapeDtypeStruct(queries.shape, jnp.bfloat16)
-    return inside_call(attend_kernel, lengths, [queries, *memories], out, limit=12)
+    return call(attend_kernel, lengths, [queries, *memories], [], out, limit=12)
 
 
 def body(pool_rows, pool_weight, lengths, owner):
@@ -177,18 +227,24 @@
     pos = jnp.stack([x, zh, y, zl]).astype(jnp.int32)
     held = [(w, *y0, *f0), (u1, *y1, *f1), (u2, *y2, *f2), (u3, *y3, *f3)]
     sums = jax.ShapeDtypeStruct((mem_g, width), jnp.float32)
-    rows, acc = inside_call(
+    buf = pltpu.VMEM((2, 4, depth, width), jnp.bfloat16)
+    rows, acc = call(
         near_kernel,
         pos,
+        [],
         [mine, *x0, other, *x1, *held[0], *held[1]],
         [jax.ShapeDtypeStruct((mem_g, model), jnp.bfloat16), sums],
-    )
-    cached = inside_call(
+        [buf, pltpu.SemaphoreType.DMA((8,)), pltpu.SemaphoreType.DMA((10,))],
+        limit=60,
+    )
+    cached = call(
         far_kernel,
         pos,
-        [rows, acc, *held[2], *held[3]],
+        [rows, acc],
+        [*held[2], *held[3]],
         jax.ShapeDtypeStruct((mem_g, width), jnp.bfloat16),
-        scratch=[pltpu.VMEM((mem_g, width), jnp.float32)],
+        [pltpu.VMEM((mem_g, width), jnp.float32), buf, pltpu.SemaphoreType.DMA((10,))],
+        limit=60,
     )
     first = cached[:, :wide]
 
@@ -205,23 +261,34 @@
     memories = [exchange(blocks[j], flips[j]) for j in range(requests)]
     attended = attend(first, memories, served)
 
-    parts = inside_call(
+    half_sum = jax.ShapeDtypeStruct((mem_g, width), jnp.bfloat16)
+    *parts, own_part = call(
         spread_kernel,
         pos,
-        [attended, *held[0], *held[1], *held[2], *held[3]],
-        jax.ShapeDtypeStruct((4, mem_g, width), jnp.bfloat16),
+        [attended],
+        [*held[0], *held[1], *held[2], *held[3]],
+        [half_sum] * 3 + [sums],
+        [pltpu.VMEM((4, 4 * depth, wide), jnp.bfloat16), pltpu.SemaphoreType.DMA((4,))],
+        limit=60,
     )
     got = []
-    for by in (2, 1, 3):
+    for part, by in zip(parts, (2, 1, 3)):
         pairs = [(4 + i, 4 + (i + by) % 4) for i in range(4)]
-        got.append(lax.ppermute(parts[by], ("side", "x"), pairs))
-    partial = parts[0].astype(jnp.float32)
-    for g in got:
-        partial = partial + g.astype(jnp.float32)
-    low, high = partial[:, :wide], partial[:, wide:]
-    give = jnp.where(zh == 0, high, low).astype(jnp.bfloat16)
+        got.append(lax.ppermute(part, ("side", "x"), pairs))
+    keep, give = call(
+        collect_kernel,
+        pos,
+        [own_part],
+        got,
+        [
+            jax.ShapeDtypeStruct((mem_g, wide), jnp.float32),
+            jax.ShapeDtypeStruct((mem_g, wide), jnp.bfloat16),
+        ],
+        [pltpu.VMEM((3, mem_g, width), jnp.bfloat16), pltpu.SemaphoreType.DMA((3,))],
+        limit=16,
+    )
     taken = lax.ppermute(give, ("side", "zh"), [(2, 3), (3, 2)])
-    decoded = (jnp.where(zh == 0, low, high) + taken.astype(jnp.float32)).astype(jnp.bfloat16)
+    decoded = (keep + taken.astype(jnp.float32)).astype(jnp.bfloat16)
     return jnp.where(side == 0, first, decoded)[None]
 
 

time: 250 us -> 233 us (0.932)
  the two profiles are of different devices: /device:TPU:17 before, /device:TPU:19 now
where the time goes in v1:
time: 233 us; the launch traced here: 232 us
  waiting for transfers between devices  137 us (59%)
  starting transfers between devices  42.6 us (18%)
  Pallas kernels  24.6 us (11%)
  local copies, waits for them, and re-layouts  15 us (6%)
  between operations  9.53 us (4%)
  other arithmetic  3.69 us (2%)
    ppermute x3, waiting for transfers between devices, route(): return lambda b: lax.ppermute(b, ('side', 'y', 'zl'), pairs)  39.5 us
    ppermute x22, waiting for transfers between devices, ring(): lax.ppermute(value, axis, [(i, (i + by) % count) for i in range(count)])  37.3 us
    ppermute x3, waiting for transfers between devices, ring_swap(): return lax.ppermute(value, 'zl', [(i, i ^ bit) for i in range(4)])  28.7 us
    pallas_call x5, Pallas kernels, call(): pl.pallas_call(kernel, out_shape=outs, in_specs=[pl.BlockSpec(memory_spac...  24.6 us
    ppermute x22, starting transfers between devices, ring(): lax.ppermute(value, axis, [(i, (i + by) % count) for i in range(count)])  17.3 us
    ppermute x3, waiting for transfers between devices, body(): got.append(lax.ppermute(part, ('side', 'x'), pairs))  14 us
    ppermute x1, waiting for transfers between devices, body(): taken = lax.ppermute(give, ('side', 'zh'), [(2, 3), (3, 2)])  11.3 us
    ppermute x3, starting transfers between devices, body(): got.append(lax.ppermute(part, ('side', 'x'), pairs))  9.02 us
  transfers between devices with their start and end apart: 33, of which 16 were waited for; matrix products, arithmetic and copies ran while one was open for 5% of the time, Pallas kernels for 3%

profile of v1, /device:TPU:19, one launch (start us, length us, event | category | flops | bytes accessed | tf_op | source)
XLA Modules:
  0.0 232.3 jit_solution(10617245479482732581)
XLA Ops:
  0.0 6.9 %collective-permute-start.51 = (bf16[48,4096]{1,0:T(8,128)(2,1)}, bf16[48,4096]{1,0:T(8,128)(2,1)}, u32[]{:S(2)}, u32[]{:S(2)}) collective-permute-start(bf16[48,4096]{1,0:T(8,128)(2,1)} %bitcast.26), channel_id=1, source_target_pairs={{0,1},{1,0},{2,3},{3,2},{4,5},{5,4},{6,7},{7,6},{8,9},{9,8},{10,11... | collective-permute-start | bytes 1179656 | tf_op jit(solution)/shard_map/ppermute | solution.py:217
  6.9 1.2 collective-permute-start.64
  9.8 1.2 collective-permute-start.48
  11.1 6.1 %collective-permute-done.51.refs_4_ = bf16[48,4096]{1,0:T(8,128)(2,1)} collective-permute-done((bf16[48,4096]{1,0:T(8,128)(2,1)}, bf16[48,4096]{1,0:T(8,128)(2,1)}, u32[]{:S(2)}, u32[]{:S(2)}) %collective-permute-start.51) | collective-permute-done | bytes 393248 | tf_op jit(solution)/shard_map/ppermute | solution.py:217
  17.4 1.6 collective-permute-done.48.refs_1_
  19.5 28.7 %collective-permute-done.64.refs_0_.refs_10_ = bf16[256,1024]{1,0:T(8,128)(2,1)S(1)} collective-permute-done((bf16[256,1024]{1,0:T(8,128)(2,1)}, bf16[256,1024]{1,0:T(8,128)(2,1)S(1)}, u32[]{:S(2)}, u32[]{:S(2)}) %collective-permute-start.64) | collective-permute-done | bytes 524320 | tf_op jit(solution)/shard_map/ppermute | solution.py:20
  48.2 1.1 collective-permute-start.60
  49.3 1.8 collective-permute-start.50
  51.4 9.5 %collective-permute-done.50.refs_3_ = bf16[48,4096]{1,0:T(8,128)(2,1)S(1)} collective-permute-done((bf16[48,4096]{1,0:T(8,128)(2,1)}, bf16[48,4096]{1,0:T(8,128)(2,1)S(1)}, u32[]{:S(2)}, u32[]{:S(2)}) %collective-permute-start.50) | collective-permute-done | bytes 393248 | tf_op jit(solution)/shard_map/ppermute | solution.py:16
  61.3 1.0 collective-permute-start.65
  62.3 4.5 %collective-permute-done.57.refs_11_.refs_3_ = bf16[128,1024]{1,0:T(8,128)(2,1)S(1)} collective-permute-done((bf16[128,1024]{1,0:T(8,128)(2,1)S(1)}, bf16[128,1024]{1,0:T(8,128)(2,1)S(1)}, u32[]{:S(2)}, u32[]{:S(2)}) %collective-permute-start.57) | collective-permute-done | bytes 262176 | tf_op jit(solution)/shard_map/ppermute | solution.py:16
  67.0 1.3 collective-permute-start.70
  68.6 4.0 %collective-permute-done.61.refs_15_.refs_7_ = bf16[256,1024]{1,0:T(8,128)(2,1)S(1)} collective-permute-done((bf16[256,1024]{1,0:T(8,128)(2,1)S(1)}, bf16[256,1024]{1,0:T(8,128)(2,1)S(1)}, u32[]{:S(2)}, u32[]{:S(2)}) %collective-permute-start.61) | collective-permute-done | bytes 524320 | tf_op jit(solution)/shard_map/ppermute | solution.py:16
  72.7 1.2 collective-permute-start.52
  73.9 4.2 %collective-permute-done.65.refs_1_.refs_11_ = bf16[256,1024]{1,0:T(8,128)(2,1)S(1)} collective-permute-done((bf16[256,1024]{1,0:T(8,128)(2,1)S(1)}, bf16[256,1024]{1,0:T(8,128)(2,1)S(1)}, u32[]{:S(2)}, u32[]{:S(2)}) %collective-permute-start.65) | collective-permute-done | bytes 524320 | tf_op jit(solution)/shard_map/ppermute | solution.py:16
  78.3 5.7 %collective-permute-done.66.refs_2_.refs_12_ = bf16[256,1024]{1,0:T(8,128)(2,1)S(1)} collective-permute-done((bf16[256,1024]{1,0:T(8,128)(2,1)S(1)}, bf16[256,1024]{1,0:T(8,128)(2,1)S(1)}, u32[]{:S(2)}, u32[]{:S(2)}) %collective-permute-start.66) | collective-permute-done | bytes 524320 | tf_op jit(solution)/shard_map/ppermute | solution.py:16
  84.0 1.8 collective-permute-start.54
  87.3 2.1 collective-permute-done.70.refs_6_.refs_16_
  89.6 5.6 %collective-permute-done.71.refs_7_.refs_17_ = bf16[256,1024]{1,0:T(8,128)(2,1)S(1)} collective-permute-done((bf16[256,1024]{1,0:T(8,128)(2,1)S(1)}, bf16[256,1024]{1,0:T(8,128)(2,1)S(1)}, u32[]{:S(2)}, u32[]{:S(2)}) %collective-permute-start.71) | collective-permute-done | bytes 524320 | tf_op jit(solution)/shard_map/ppermute | solution.py:16
  95.2 1.6 collective-permute-start.62
  97.8 1.7 slice.73
  102.5 1.5 collective-permute-start.67
  104.0 1.4 collective-permute-start.72
  116.0 1.9 pad_add_fusion.1.lengths_ref
  119.3 7.8 %shard_map.46 = (bf16[384,4096]{1,0:T(8,128)(2,1)}, f32[384,1024]{1,0:T(8,128)}) custom-call(s32[4]{0:T(128)} %pad_add_fusion.pos_ref, bf16[48,4096]{1,0:T(8,128)(2,1)} %bitcast.30, bf16[48,4096]{1,0:T(8,128)(2,1)} %copy-done.21, bf16[48,4096]{1,0:T(8,128)(2,1)} %copy-done.22, bf16[48,4096]{1,0:T(8,128)(2,1)} %copy-done.23, ...), custom_call_target="tpu_custom_call" | custom-call | tf_op jit(solution)/shard_map/pallas_call | solution.py:150
  128.2 6.6 %shard_map.47 = bf16[384,1024]{1,0:T(8,128)(2,1)} custom-call(s32[4]{0:T(128)} %pad_add_fusion.pos_ref, bf16[384,4096]{1,0:T(8,128)(2,1)} %get-tuple-element.112.rows_ref, f32[384,1024]{1,0:T(8,128)} %get-tuple-element.113.sum_ref, bf16[256,1024]{1,0:T(8,128)(2,1)} %copy-done.12, bf16[256,1024]{1,0:T(8,128)(2,1)} %copy-done.4, bf16[256,1024]{1,0:T(8,128)(2,1)} %copy-done.5, ...), custom_call_target="tpu_custom_call" | custom-call | tf_op jit(solution)/shard_map/pallas_call | solution.py:150
  134.8 1.0 slice.78.queries_ref
  135.8 1.8 pad_dynamic-slice_fusion
  137.6 16.1 %conditional.3 = (bf16[192,1024]{1,0:T(8,128)(2,1)}) conditional(s32[]{:T(128)} %clamp.9, bf16[192,1024]{1,0:T(8,128)(2,1)S(1)} %get-tuple-element.122, bf16[192,1024]{1,0:T(8,128)(2,1)S(1)} %get-tuple-element.122, bf16[192,1024]{1,0:T(8,128)(2,1)S(1)} %get-tuple-element.122, ...), branch_computations={%region_1.2_spmd, %region_2.3_spmd, %region_3.4_spmd, %region_4.5_... | conditional | bytes 1572912 | solution.py:30
  137.7 1.3 collective-permute-start.15
  139.0 14.7 %collective-permute-done.15 = bf16[192,1024]{1,0:T(8,128)(2,1)} collective-permute-done((bf16[192,1024]{1,0:T(8,128)(2,1)S(1)}, bf16[192,1024]{1,0:T(8,128)(2,1)}, u32[]{:S(2)}, u32[]{:S(2)}) %collective-permute-start.15) | collective-permute-done | bytes 393248 | tf_op jit(solution)/shard_map/cond/branch_15_fun/ppermute | solution.py:28
  153.7 10.7 %conditional.4 = (bf16[192,1024]{1,0:T(8,128)(2,1)}) conditional(s32[]{:T(128)} %clamp.10, bf16[192,1024]{1,0:T(8,128)(2,1)S(1)} %get-tuple-element.121, bf16[192,1024]{1,0:T(8,128)(2,1)S(1)} %get-tuple-element.121, bf16[192,1024]{1,0:T(8,128)(2,1)S(1)} %get-tuple-element.121, ...), branch_computations={%region_17.18_spmd, %region_18.19_spmd, %region_19.20_spmd, %regio... | conditional | bytes 1572912 | solution.py:30
  153.7 1.3 collective-permute-start.24
  155.0 9.4 %collective-permute-done.24 = bf16[192,1024]{1,0:T(8,128)(2,1)} collective-permute-done((bf16[192,1024]{1,0:T(8,128)(2,1)S(1)}, bf16[192,1024]{1,0:T(8,128)(2,1)}, u32[]{:S(2)}, u32[]{:S(2)}) %collective-permute-start.24) | collective-permute-done | bytes 393248 | tf_op jit(solution)/shard_map/cond/branch_8_fun/ppermute | solution.py:28
  164.4 16.7 %conditional.5 = (bf16[192,1024]{1,0:T(8,128)(2,1)}) conditional(s32[]{:T(128)} %clamp.11, bf16[192,1024]{1,0:T(8,128)(2,1)S(1)} %get-tuple-element.120, bf16[192,1024]{1,0:T(8,128)(2,1)S(1)} %get-tuple-element.120, bf16[192,1024]{1,0:T(8,128)(2,1)S(1)} %get-tuple-element.120, ...), branch_computations={%region_33.34_spmd, %region_34.35_spmd, %region_35.36_spmd, %regio... | conditional | bytes 1572912 | solution.py:30
  164.4 1.3 collective-permute-start.46
  165.7 15.4 %collective-permute-done.46 = bf16[192,1024]{1,0:T(8,128)(2,1)} collective-permute-done((bf16[192,1024]{1,0:T(8,128)(2,1)S(1)}, bf16[192,1024]{1,0:T(8,128)(2,1)}, u32[]{:S(2)}, u32[]{:S(2)}) %collective-permute-start.46) | collective-permute-done | bytes 393248 | tf_op jit(solution)/shard_map/cond/branch_14_fun/ppermute | solution.py:28
  181.1 2.7 %shard_map.48.attended_ref = bf16[384,512]{1,0:T(8,128)(2,1)S(1)} custom-call(s32[3]{0:T(128)S(1)} %pad_add_fusion.1.lengths_ref, bf16[384,512]{1,0:T(8,128)(2,1)S(1)} %slice.78.queries_ref, bf16[192,1024]{1,0:T(8,128)(2,1)} %get-tuple-element.132.refs_0_, bf16[192,1024]{1,0:T(8,128)(2,1)} %get-tuple-element.133.refs_1_, ...), custom_call_target="tpu_custom_call" | custom-call | tf_op jit(solution)/shard_map/pallas_call | solution.py:150
  184.6 6.0 %shard_map.49 = (bf16[384,1024]{1,0:T(8,128)(2,1)}, bf16[384,1024]{1,0:T(8,128)(2,1)}, bf16[384,1024]{1,0:T(8,128)(2,1)}, f32[384,1024]{1,0:T(8,128)}) custom-call(s32[4]{0:T(128)} %pad_add_fusion.pos_ref, bf16[384,512]{1,0:T(8,128)(2,1)} %copy-done, bf16[256,1024]{1,0:T(8,128)(2,1)} %bitcast.25, bf16[256,1024]{1,0:T(8,128)(2,1)} %copy-done.8, ...), custom_call_target="tpu_custom_call" | custom-call | tf_op jit(solution)/shard_map/pallas_call | solution.py:150
  190.5 3.7 %collective-permute-start.74 = (bf16[384,1024]{1,0:T(8,128)(2,1)}, bf16[384,1024]{1,0:T(8,128)(2,1)S(1)}, u32[]{:S(2)}, u32[]{:S(2)}) collective-permute-start(bf16[384,1024]{1,0:T(8,128)(2,1)} %get-tuple-element.115), channel_id=1, source_target_pairs={{128,132},{130,134},{132,128},{134,130},{129,133},{131,135},{133,1... | collective-permute-start | bytes 2359304 | tf_op jit(solution)/shard_map/ppermute | solution.py:277
  194.3 1.9 collective-permute-start.75
  196.2 3.4 %collective-permute-start.76 = (bf16[384,1024]{1,0:T(8,128)(2,1)}, bf16[384,1024]{1,0:T(8,128)(2,1)S(1)}, u32[]{:S(2)}, u32[]{:S(2)}) collective-permute-start(bf16[384,1024]{1,0:T(8,128)(2,1)} %get-tuple-element.117), channel_id=1, source_target_pairs={{128,134},{130,128},{132,130},{134,132},{129,135},{131,129},{133,1... | collective-permute-start | bytes 2359304 | tf_op jit(solution)/shard_map/ppermute | solution.py:277
  199.6 5.5 %collective-permute-done.74.refs_0_ = bf16[384,1024]{1,0:T(8,128)(2,1)S(1)} collective-permute-done((bf16[384,1024]{1,0:T(8,128)(2,1)}, bf16[384,1024]{1,0:T(8,128)(2,1)S(1)}, u32[]{:S(2)}, u32[]{:S(2)}) %collective-permute-start.74) | collective-permute-done | bytes 786464 | tf_op jit(solution)/shard_map/ppermute | solution.py:277
  205.1 8.5 %collective-permute-done.75.refs_1_ = bf16[384,1024]{1,0:T(8,128)(2,1)S(1)} collective-permute-done((bf16[384,1024]{1,0:T(8,128)(2,1)}, bf16[384,1024]{1,0:T(8,128)(2,1)S(1)}, u32[]{:S(2)}, u32[]{:S(2)}) %collective-permute-start.75) | collective-permute-done | bytes 786464 | tf_op jit(solution)/shard_map/ppermute | solution.py:277
  213.6 1.4 copy-done.1
  215.0 1.5 shard_map.50
  216.5 3.5 %collective-permute-start.77 = (bf16[384,512]{1,0:T(8,128)(2,1)S(1)}, bf16[384,512]{1,0:T(8,128)(2,1)S(1)}, u32[]{:S(2)}, u32[]{:S(2)}) collective-permute-start(bf16[384,512]{1,0:T(8,128)(2,1)S(1)} %get-tuple-element.119), channel_id=1, source_target_pairs={{128,129},{129,128},{130,131},{131,130},{132,133},{133,132},{134,1... | collective-permute-start | bytes 1179656 | tf_op jit(solution)/shard_map/ppermute | solution.py:290
  220.1 11.3 %collective-permute-done.77 = bf16[384,512]{1,0:T(8,128)(2,1)S(1)} collective-permute-done((bf16[384,512]{1,0:T(8,128)(2,1)S(1)}, bf16[384,512]{1,0:T(8,128)(2,1)S(1)}, u32[]{:S(2)}, u32[]{:S(2)}) %collective-permute-start.77) | collective-permute-done | bytes 393248 | tf_op jit(solution)/shard_map/ppermute | solution.py:290
  (97 shorter events, 15.0 us)
Async XLA Ops:
  0.0 96.8 %copy-start.25 = (s32[16,3]{0,1:T(4,128)S(1)}, s32[16,3]{0,1:T(4,128)}, u32[]{:S(2)}) copy-start(s32[16,3]{0,1:T(4,128)} %param.55) | copy-start | bytes 580
  0.0 97.4 %copy-start.24 = (s32[16,3]{0,1:T(4,128)S(1)}, s32[16,3]{0,1:T(4,128)}, u32[]{:S(2)}) copy-start(s32[16,3]{0,1:T(4,128)} %param.54) | copy-start | bytes 580
  0.0 17.2 %collective-permute-start.51 = (bf16[48,4096]{1,0:T(8,128)(2,1)}, bf16[48,4096]{1,0:T(8,128)(2,1)}, u32[]{:S(2)}, u32[]{:S(2)}) collective-permute-start(bf16[48,4096]{1,0:T(8,128)(2,1)} %bitcast.26), channel_id=1, source_target_pairs={{0,1},{1,0},{2,3},{3,2},{4,5},{5,4},{6,7},{7,6},{8,9},{9,8},{10,11... | collective-permute-start | bytes 1179656 | tf_op jit(solution)/shard_map/ppermute | solution.py:217
  6.9 41.3 %collective-permute-start.64 = (bf16[256,1024]{1,0:T(8,128)(2,1)}, bf16[256,1024]{1,0:T(8,128)(2,1)S(1)}, u32[]{:S(2)}, u32[]{:S(2)}) collective-permute-start(bf16[256,1024]{1,0:T(8,128)(2,1)} %bitcast.20), channel_id=1, source_target_pairs={{0,16},{8,24},{16,0},{24,8},{1,17},{9,25},{17,1},{25,9},{2,18},{10... | collective-permute-start | bytes 1572872 | tf_op jit(solution)/shard_map/ppermute | solution.py:20
  8.1 40.1 %collective-permute-start.59 = (bf16[256,1024]{1,0:T(8,128)(2,1)}, bf16[256,1024]{1,0:T(8,128)(2,1)S(1)}, u32[]{:S(2)}, u32[]{:S(2)}) collective-permute-start(bf16[256,1024]{1,0:T(8,128)(2,1)} %bitcast.21), channel_id=1, source_target_pairs={{0,8},{8,0},{16,24},{24,16},{1,9},{9,1},{17,25},{25,17},{2,10},{10... | collective-permute-start | bytes 1572872 | tf_op jit(solution)/shard_map/ppermute | solution.py:20
  8.8 40.4 %collective-permute-start.55 = (bf16[256,1024]{1,0:T(8,128)(2,1)}, bf16[256,1024]{1,0:T(8,128)(2,1)S(1)}, u32[]{:S(2)}, u32[]{:S(2)}) collective-permute-start(bf16[256,1024]{1,0:T(8,128)(2,1)} %bitcast.22), channel_id=1, source_target_pairs={{0,32},{32,64},{64,96},{96,0},{1,33},{33,65},{65,97},{97,1},{2,34}... | collective-permute-start | bytes 1572872 | tf_op jit(solution)/shard_map/ppermute | solution.py:16
  9.8 9.2 %collective-permute-start.48 = (bf16[48,4096]{1,0:T(8,128)(2,1)}, bf16[48,4096]{1,0:T(8,128)(2,1)S(1)}, u32[]{:S(2)}, u32[]{:S(2)}) collective-permute-start(bf16[48,4096]{1,0:T(8,128)(2,1)} %bitcast.27), channel_id=1, source_target_pairs={{0,2},{2,4},{4,6},{6,0},{1,3},{3,5},{5,7},{7,1},{8,10},{10,12},{12... | collective-permute-start | bytes 1179656 | tf_op jit(solution)/shard_map/ppermute | solution.py:16
  17.2 34.0 %collective-permute-start.49 = (bf16[48,4096]{1,0:T(8,128)(2,1)}, bf16[48,4096]{1,0:T(8,128)(2,1)S(1)}, u32[]{:S(2)}, u32[]{:S(2)}) collective-permute-start(bf16[48,4096]{1,0:T(8,128)(2,1)} %bitcast.28), channel_id=1, source_target_pairs={{0,6},{2,0},{4,2},{6,4},{1,7},{3,1},{5,3},{7,5},{8,14},{10,8},{12,... | collective-permute-start | bytes 1179656 | tf_op jit(solution)/shard_map/ppermute | solution.py:16
  19.0 32.1 %copy-start.21 = (bf16[48,4096]{1,0:T(8,128)(2,1)}, bf16[48,4096]{1,0:T(8,128)(2,1)S(1)}, u32[]{:S(2)}) copy-start(bf16[48,4096]{1,0:T(8,128)(2,1)S(1)} %collective-permute-done.48.refs_1_) | copy-start | bytes 1179652
  19.0 42.3 %collective-permute-start.56 = (bf16[256,1024]{1,0:T(8,128)(2,1)}, bf16[256,1024]{1,0:T(8,128)(2,1)S(1)}, u32[]{:S(2)}, u32[]{:S(2)}) collective-permute-start(bf16[256,1024]{1,0:T(8,128)(2,1)} %bitcast.23), channel_id=1, source_target_pairs={{0,96},{32,0},{64,32},{96,64},{1,97},{33,1},{65,33},{97,65},{2,98}... | collective-permute-start | bytes 1572872 | tf_op jit(solution)/shard_map/ppermute | solution.py:16
  48.2 48.6 %copy-start.12 = (bf16[256,1024]{1,0:T(8,128)(2,1)}, bf16[256,1024]{1,0:T(8,128)(2,1)S(1)}, u32[]{:S(2)}) copy-start(bf16[256,1024]{1,0:T(8,128)(2,1)S(1)} %collective-permute-done.64.refs_0_.refs_10_) | copy-start | bytes 1572868
  48.2 18.8 %collective-permute-start.69 = (bf16[256,1024]{1,0:T(8,128)(2,1)S(1)}, bf16[256,1024]{1,0:T(8,128)(2,1)S(1)}, u32[]{:S(2)}, u32[]{:S(2)}) collective-permute-start(bf16[256,1024]{1,0:T(8,128)(2,1)S(1)} %collective-permute-done.64.refs_0_.refs_10_), channel_id=1, source_target_pairs={{0,8},{8,0},{16,24},{24,16},{1,9},{9,1},{17,25},{25,17},{2,10},{10... | collective-permute-start | bytes 1572872 | tf_op jit(solution)/shard_map/ppermute | solution.py:20
  48.2 49.2 %copy-start.14 = (bf16[256,1024]{1,0:T(8,128)(2,1)}, bf16[256,1024]{1,0:T(8,128)(2,1)S(1)}, u32[]{:S(2)}) copy-start(bf16[256,1024]{1,0:T(8,128)(2,1)S(1)} %collective-permute-done.59.refs_13_.refs_5_) | copy-start | bytes 1572868
  48.2 20.1 %collective-permute-start.60 = (bf16[256,1024]{1,0:T(8,128)(2,1)S(1)}, bf16[256,1024]{1,0:T(8,128)(2,1)S(1)}, u32[]{:S(2)}, u32[]{:S(2)}) collective-permute-start(bf16[256,1024]{1,0:T(8,128)(2,1)S(1)} %collective-permute-done.59.refs_13_.refs_5_), channel_id=1, source_target_pairs={{0,32},{32,64},{64,96},{96,0},{1,33},{33,65},{65,97},{97,1},{2,34}... | collective-permute-start | bytes 1572872 | tf_op jit(solution)/shard_map/ppermute | solution.py:16
  49.3 51.7 %copy-start.8 = (bf16[256,1024]{1,0:T(8,128)(2,1)}, bf16[256,1024]{1,0:T(8,128)(2,1)S(1)}, u32[]{:S(2)}) copy-start(bf16[256,1024]{1,0:T(8,128)(2,1)S(1)} %collective-permute-done.55.refs_9_.refs_1_) | copy-start | bytes 1572868
  49.3 11.6 %collective-permute-start.50 = (bf16[48,4096]{1,0:T(8,128)(2,1)}, bf16[48,4096]{1,0:T(8,128)(2,1)S(1)}, u32[]{:S(2)}, u32[]{:S(2)}) collective-permute-start(bf16[48,4096]{1,0:T(8,128)(2,1)} %bitcast.29), channel_id=1, source_target_pairs={{0,4},{2,6},{4,0},{6,2},{1,5},{3,7},{5,1},{7,3},{8,12},{10,14},{12... | collective-permute-start | bytes 1179656 | tf_op jit(solution)/shard_map/ppermute | solution.py:16
  51.2 46.2 %copy-start.22 = (bf16[48,4096]{1,0:T(8,128)(2,1)}, bf16[48,4096]{1,0:T(8,128)(2,1)S(1)}, u32[]{:S(2)}) copy-start(bf16[48,4096]{1,0:T(8,128)(2,1)S(1)} %collective-permute-done.49.refs_2_) | copy-start | bytes 1179652
  51.2 15.6 %collective-permute-start.57 = (bf16[128,1024]{1,0:T(8,128)(2,1)S(1)}, bf16[128,1024]{1,0:T(8,128)(2,1)S(1)}, u32[]{:S(2)}, u32[]{:S(2)}) collective-permute-start(bf16[128,1024]{1,0:T(8,128)(2,1)S(1)} %slice.70), channel_id=1, source_target_pairs={{0,32},{32,64},{64,96},{96,0},{1,33},{33,65},{65,97},{97,1},{2,34}... | collective-permute-start | bytes 786440 | tf_op jit(solution)/shard_map/ppermute | solution.py:16
  60.9 36.5 %copy-start.23 = (bf16[48,4096]{1,0:T(8,128)(2,1)}, bf16[48,4096]{1,0:T(8,128)(2,1)S(1)}, u32[]{:S(2)}) copy-start(bf16[48,4096]{1,0:T(8,128)(2,1)S(1)} %collective-permute-done.50.refs_3_) | copy-start | bytes 1179652
  60.9 11.8 %collective-permute-start.61 = (bf16[256,1024]{1,0:T(8,128)(2,1)S(1)}, bf16[256,1024]{1,0:T(8,128)(2,1)S(1)}, u32[]{:S(2)}, u32[]{:S(2)}) collective-permute-start(bf16[256,1024]{1,0:T(8,128)(2,1)S(1)} %collective-permute-done.59.refs_13_.refs_5_), channel_id=1, source_target_pairs={{0,96},{32,0},{64,32},{96,64},{1,97},{33,1},{65,33},{97,65},{2,98}... | collective-permute-start | bytes 1572872 | tf_op jit(solution)/shard_map/ppermute | solution.py:16
  61.3 40.4 %copy-start.9 = (bf16[256,1024]{1,0:T(8,128)(2,1)}, bf16[256,1024]{1,0:T(8,128)(2,1)S(1)}, u32[]{:S(2)}) copy-start(bf16[256,1024]{1,0:T(8,128)(2,1)S(1)} %collective-permute-done.56.refs_10_.refs_2_) | copy-start | bytes 1572868
  61.3 16.7 %collective-permute-start.65 = (bf16[256,1024]{1,0:T(8,128)(2,1)S(1)}, bf16[256,1024]{1,0:T(8,128)(2,1)S(1)}, u32[]{:S(2)}, u32[]{:S(2)}) collective-permute-start(bf16[256,1024]{1,0:T(8,128)(2,1)S(1)} %collective-permute-done.64.refs_0_.refs_10_), channel_id=1, source_target_pairs={{0,32},{32,64},{64,96},{96,0},{1,33},{33,65},{65,97},{97,1},{2,34}... | collective-permute-start | bytes 1572872 | tf_op jit(solution)/shard_map/ppermute | solution.py:16
  66.8 51.8 %copy-start.19 = (bf16[128,1024]{1,0:T(8,128)(2,1)}, bf16[128,1024]{1,0:T(8,128)(2,1)S(1)}, u32[]{:S(2)}) copy-start(bf16[128,1024]{1,0:T(8,128)(2,1)S(1)} %collective-permute-done.57.refs_11_.refs_3_) | copy-start | bytes 786436
  66.8 17.2 %collective-permute-start.66 = (bf16[256,1024]{1,0:T(8,128)(2,1)S(1)}, bf16[256,1024]{1,0:T(8,128)(2,1)S(1)}, u32[]{:S(2)}, u32[]{:S(2)}) collective-permute-start(bf16[256,1024]{1,0:T(8,128)(2,1)S(1)} %collective-permute-done.64.refs_0_.refs_10_), channel_id=1, source_target_pairs={{0,96},{32,0},{64,32},{96,64},{1,97},{33,1},{65,33},{97,65},{2,98}... | collective-permute-start | bytes 1572872 | tf_op jit(solution)/shard_map/ppermute | solution.py:16
  67.0 30.4 %copy-start.13 = (bf16[256,1024]{1,0:T(8,128)(2,1)}, bf16[256,1024]{1,0:T(8,128)(2,1)S(1)}, u32[]{:S(2)}) copy-start(bf16[256,1024]{1,0:T(8,128)(2,1)S(1)} %collective-permute-done.69.refs_5_.refs_15_) | copy-start | bytes 1572868
  67.0 22.4 %collective-permute-start.70 = (bf16[256,1024]{1,0:T(8,128)(2,1)S(1)}, bf16[256,1024]{1,0:T(8,128)(2,1)S(1)}, u32[]{:S(2)}, u32[]{:S(2)}) collective-permute-start(bf16[256,1024]{1,0:T(8,128)(2,1)S(1)} %collective-permute-done.69.refs_5_.refs_15_), channel_id=1, source_target_pairs={{0,32},{32,64},{64,96},{96,0},{1,33},{33,65},{65,97},{97,1},{2,34}... | collective-permute-start | bytes 1572872 | tf_op jit(solution)/shard_map/ppermute | solution.py:16
  68.3 26.9 %copy-start.10 = (bf16[256,1024]{1,0:T(8,128)(2,1)}, bf16[256,1024]{1,0:T(8,128)(2,1)S(1)}, u32[]{:S(2)}) copy-start(bf16[256,1024]{1,0:T(8,128)(2,1)S(1)} %collective-permute-done.60.refs_14_.refs_6_) | copy-start | bytes 1572868
  68.3 26.9 %collective-permute-start.71 = (bf16[256,1024]{1,0:T(8,128)(2,1)S(1)}, bf16[256,1024]{1,0:T(8,128)(2,1)S(1)}, u32[]{:S(2)}, u32[]{:S(2)}) collective-permute-start(bf16[256,1024]{1,0:T(8,128)(2,1)S(1)} %collective-permute-done.69.refs_5_.refs_15_), channel_id=1, source_target_pairs={{0,96},{32,0},{64,32},{96,64},{1,97},{33,1},{65,33},{97,65},{2,98}... | collective-permute-start | bytes 1572872 | tf_op jit(solution)/shard_map/ppermute | solution.py:16
  72.7 29.8 %collective-permute-start.52 = (bf16[48,4096]{1,0:T(8,128)(2,1)}, bf16[48,4096]{1,0:T(8,128)(2,1)}, u32[]{:S(2)}, u32[]{:S(2)}) collective-permute-start(bf16[48,4096]{1,0:T(8,128)(2,1)} %collective-permute-done.51.refs_4_), channel_id=1, source_target_pairs={{0,2},{2,4},{4,6},{6,0},{1,3},{3,5},{5,7},{7,1},{8,10},{10,12},{12... | collective-permute-start | bytes 1179656 | tf_op jit(solution)/shard_map/ppermute | solution.py:16
  78.1 25.9 %collective-permute-start.53 = (bf16[48,4096]{1,0:T(8,128)(2,1)}, bf16[48,4096]{1,0:T(8,128)(2,1)}, u32[]{:S(2)}, u32[]{:S(2)}) collective-permute-start(bf16[48,4096]{1,0:T(8,128)(2,1)} %collective-permute-done.51.refs_4_), channel_id=1, source_target_pairs={{0,6},{2,0},{4,2},{6,4},{1,7},{3,1},{5,3},{7,5},{8,14},{10,8},{12,... | collective-permute-start | bytes 1179656 | tf_op jit(solution)/shard_map/ppermute | solution.py:16
  84.0 20.0 %collective-permute-start.54 = (bf16[48,4096]{1,0:T(8,128)(2,1)}, bf16[48,4096]{1,0:T(8,128)(2,1)}, u32[]{:S(2)}, u32[]{:S(2)}) collective-permute-start(bf16[48,4096]{1,0:T(8,128)(2,1)} %collective-permute-done.51.refs_4_), channel_id=1, source_target_pairs={{0,4},{2,6},{4,0},{6,2},{1,5},{3,7},{5,1},{7,3},{8,12},{10,14},{12... | collective-permute-start | bytes 1179656 | tf_op jit(solution)/shard_map/ppermute | solution.py:16
  89.4 37.8 %copy-start.6 = (bf16[256,1024]{1,0:T(8,128)(2,1)}, bf16[256,1024]{1,0:T(8,128)(2,1)S(1)}, u32[]{:S(2)}) copy-start(bf16[256,1024]{1,0:T(8,128)(2,1)S(1)} %collective-permute-done.70.refs_6_.refs_16_) | copy-start | bytes 1572868
  89.4 13.0 %collective-permute-start.58 = (bf16[128,1024]{1,0:T(8,128)(2,1)}, bf16[128,1024]{1,0:T(8,128)(2,1)}, u32[]{:S(2)}, u32[]{:S(2)}) collective-permute-start(bf16[128,1024]{1,0:T(8,128)(2,1)} %slice.71), channel_id=1, source_target_pairs={{0,96},{32,0},{64,32},{96,64},{1,97},{33,1},{65,33},{97,65},{2,98}... | collective-permute-start | bytes 786440 | tf_op jit(solution)/shard_map/ppermute | solution.py:16
  95.2 31.9 %copy-start.7 = (bf16[256,1024]{1,0:T(8,128)(2,1)}, bf16[256,1024]{1,0:T(8,128)(2,1)S(1)}, u32[]{:S(2)}) copy-start(bf16[256,1024]{1,0:T(8,128)(2,1)S(1)} %collective-permute-done.71.refs_7_.refs_17_) | copy-start | bytes 1572868
  95.2 10.2 %collective-permute-start.62 = (bf16[128,1024]{1,0:T(8,128)(2,1)}, bf16[128,1024]{1,0:T(8,128)(2,1)}, u32[]{:S(2)}, u32[]{:S(2)}) collective-permute-start(bf16[128,1024]{1,0:T(8,128)(2,1)} %slice.72), channel_id=1, source_target_pairs={{0,32},{32,64},{64,96},{96,0},{1,33},{33,65},{65,97},{97,1},{2,34}... | collective-permute-start | bytes 786440 | tf_op jit(solution)/shard_map/ppermute | solution.py:16
  102.5 16.2 %collective-permute-start.63 = (bf16[128,1024]{1,0:T(8,128)(2,1)}, bf16[128,1024]{1,0:T(8,128)(2,1)S(1)}, u32[]{:S(2)}, u32[]{:S(2)}) collective-permute-start(bf16[128,1024]{1,0:T(8,128)(2,1)} %slice.73), channel_id=1, source_target_pairs={{0,96},{32,0},{64,32},{96,64},{1,97},{33,1},{65,33},{97,65},{2,98}... | collective-permute-start | bytes 786440 | tf_op jit(solution)/shard_map/ppermute | solution.py:16
  102.5 24.7 %collective-permute-start.67 = (bf16[128,1024]{1,0:T(8,128)(2,1)}, bf16[128,1024]{1,0:T(8,128)(2,1)S(1)}, u32[]{:S(2)}, u32[]{:S(2)}) collective-permute-start(bf16[128,1024]{1,0:T(8,128)(2,1)} %slice.74), channel_id=1, source_target_pairs={{0,32},{32,64},{64,96},{96,0},{1,33},{33,65},{65,97},{97,1},{2,34}... | collective-permute-start | bytes 786440 | tf_op jit(solution)/shard_map/ppermute | solution.py:16
  103.9 23.3 %collective-permute-start.68 = (bf16[128,1024]{1,0:T(8,128)(2,1)}, bf16[128,1024]{1,0:T(8,128)(2,1)S(1)}, u32[]{:S(2)}, u32[]{:S(2)}) collective-permute-start(bf16[128,1024]{1,0:T(8,128)(2,1)} %slice.75), channel_id=1, source_target_pairs={{0,96},{32,0},{64,32},{96,64},{1,97},{33,1},{65,33},{97,65},{2,98}... | collective-permute-start | bytes 786440 | tf_op jit(solution)/shard_map/ppermute | solution.py:16
  104.0 23.2 %collective-permute-start.72 = (bf16[128,1024]{1,0:T(8,128)(2,1)}, bf16[128,1024]{1,0:T(8,128)(2,1)S(1)}, u32[]{:S(2)}, u32[]{:S(2)}) collective-permute-start(bf16[128,1024]{1,0:T(8,128)(2,1)} %slice.76), channel_id=1, source_target_pairs={{0,32},{32,64},{64,96},{96,0},{1,33},{33,65},{65,97},{97,1},{2,34}... | collective-permute-start | bytes 786440 | tf_op jit(solution)/shard_map/ppermute | solution.py:16
  105.4 21.8 %collective-permute-start.73 = (bf16[128,1024]{1,0:T(8,128)(2,1)}, bf16[128,1024]{1,0:T(8,128)(2,1)S(1)}, u32[]{:S(2)}, u32[]{:S(2)}) collective-permute-start(bf16[128,1024]{1,0:T(8,128)(2,1)} %slice.77), channel_id=1, source_target_pairs={{0,96},{32,0},{64,32},{96,64},{1,97},{33,1},{65,33},{97,65},{2,98}... | collective-permute-start | bytes 786440 | tf_op jit(solution)/shard_map/ppermute | solution.py:16
  137.7 16.0 %collective-permute-start.15 = (bf16[192,1024]{1,0:T(8,128)(2,1)S(1)}, bf16[192,1024]{1,0:T(8,128)(2,1)}, u32[]{:S(2)}, u32[]{:S(2)}) collective-permute-start(bf16[192,1024]{1,0:T(8,128)(2,1)S(1)} %param.15), channel_id=1, source_target_pairs={{0,248},{8,240},{16,232},{24,224},{32,216},{40,208},{48,200},{56,1... | collective-permute-start | bytes 1179656 | tf_op jit(solution)/shard_map/cond/branch_15_fun/ppermute | solution.py:28
  153.7 10.7 %collective-permute-start.24 = (bf16[192,1024]{1,0:T(8,128)(2,1)S(1)}, bf16[192,1024]{1,0:T(8,128)(2,1)}, u32[]{:S(2)}, u32[]{:S(2)}) collective-permute-start(bf16[192,1024]{1,0:T(8,128)(2,1)S(1)} %param.24), channel_id=1, source_target_pairs={{0,192},{8,200},{16,208},{24,216},{32,224},{40,232},{48,240},{56,2... | collective-permute-start | bytes 1179656 | tf_op jit(solution)/shard_map/cond/branch_8_fun/ppermute | solution.py:28
  164.4 16.7 %collective-permute-start.46 = (bf16[192,1024]{1,0:T(8,128)(2,1)S(1)}, bf16[192,1024]{1,0:T(8,128)(2,1)}, u32[]{:S(2)}, u32[]{:S(2)}) collective-permute-start(bf16[192,1024]{1,0:T(8,128)(2,1)S(1)} %param.46), channel_id=1, source_target_pairs={{0,240},{8,248},{16,224},{24,232},{32,208},{40,216},{48,192},{56,2... | collective-permute-start | bytes 1179656 | tf_op jit(solution)/shard_map/cond/branch_14_fun/ppermute | solution.py:28
  184.6 29.0 %copy-start.2 = (s32[4]{0:T(128)S(1)}, s32[4]{0:T(128)}, u32[]{:S(2)}) copy-start(s32[4]{0:T(128)} %pad_add_fusion.pos_ref) | copy-start | bytes 52
  190.5 14.5 %collective-permute-start.74 = (bf16[384,1024]{1,0:T(8,128)(2,1)}, bf16[384,1024]{1,0:T(8,128)(2,1)S(1)}, u32[]{:S(2)}, u32[]{:S(2)}) collective-permute-start(bf16[384,1024]{1,0:T(8,128)(2,1)} %get-tuple-element.115), channel_id=1, source_target_pairs={{128,132},{130,134},{132,128},{134,130},{129,133},{131,135},{133,1... | collective-permute-start | bytes 2359304 | tf_op jit(solution)/shard_map/ppermute | solution.py:277
  194.3 19.3 %collective-permute-start.75 = (bf16[384,1024]{1,0:T(8,128)(2,1)}, bf16[384,1024]{1,0:T(8,128)(2,1)S(1)}, u32[]{:S(2)}, u32[]{:S(2)}) collective-permute-start(bf16[384,1024]{1,0:T(8,128)(2,1)} %get-tuple-element.116), channel_id=1, source_target_pairs={{128,130},{130,132},{132,134},{134,128},{129,131},{131,133},{133,1... | collective-permute-start | bytes 2359304 | tf_op jit(solution)/shard_map/ppermute | solution.py:277
  196.2 17.4 %collective-permute-start.76 = (bf16[384,1024]{1,0:T(8,128)(2,1)}, bf16[384,1024]{1,0:T(8,128)(2,1)S(1)}, u32[]{:S(2)}, u32[]{:S(2)}) collective-permute-start(bf16[384,1024]{1,0:T(8,128)(2,1)} %get-tuple-element.117), channel_id=1, source_target_pairs={{128,134},{130,128},{132,130},{134,132},{129,135},{131,129},{133,1... | collective-permute-start | bytes 2359304 | tf_op jit(solution)/shard_map/ppermute | solution.py:277
  216.5 14.8 %collective-permute-start.77 = (bf16[384,512]{1,0:T(8,128)(2,1)S(1)}, bf16[384,512]{1,0:T(8,128)(2,1)S(1)}, u32[]{:S(2)}, u32[]{:S(2)}) collective-permute-start(bf16[384,512]{1,0:T(8,128)(2,1)S(1)} %get-tuple-element.119), channel_id=1, source_target_pairs={{128,129},{129,128},{130,131},{131,130},{132,133},{133,132},{134,1... | collective-permute-start | bytes 1179656 | tf_op jit(solution)/shard_map/ppermute | solution.py:290
  (11 other events, 75.3 us)

commit v2 on v1

--- a/solution.py
+++ b/solution.py
@@ -217,9 +217,9 @@
     other = lax.ppermute(mine, "zh", [(0, 1), (1, 0)])
     y2 = both(u2, "y")
     f1 = further(y1)
-    y3 = both(u3, "y")
     f2 = further(y2)
     x1 = both(other, "x") + (ring(other, "x", 2),)
+    y3 = both(u3, "y")
     f3 = further(y3)
 
     mem_g = 8 * count
@@ -244,20 +244,28 @@
         [*held[2], *held[3]],
         jax.ShapeDtypeStruct((mem_g, width), jnp.bfloat16),
         [pltpu.VMEM((mem_g, width), jnp.float32), buf, pltpu.SemaphoreType.DMA((10,))],
-        limit=60,
+        limit=52,
     )
     first = cached[:, :wide]
 
     group = y * 4 + zl
     flips = owner[0]
-    own = lax.dynamic_index_in_dim(lengths, group, 0, keepdims=False)
+    own = lax.dynamic_index_in_dim(
+        lengths, group, 0, keepdims=False, allow_negative_indices=False
+    )
     begins = jnp.cumsum(own) - own
     served = jnp.concatenate(
-        [lax.dynamic_slice(lengths, (group ^ flips[j], j), (1, 1))[0] for j in range(requests)]
+        [lax.dynamic_slice(
+            lengths, (group ^ flips[j], j), (1, 1), allow_negative_indices=False
+        )[0]
+            for j in range(requests)]
     )
     begins = [begins[j] for j in range(requests)]
     padded = jnp.concatenate([cached, jnp.zeros((maxlen, width), jnp.bfloat16)], axis=0)
-    blocks = [lax.dynamic_slice(padded, (begins[j], 0), (maxlen, width)) for j in range(requests)]
+    blocks = [lax.dynamic_slice(
+        padded, (begins[j], 0), (maxlen, width), allow_negative_indices=False
+    )
+        for j in range(requests)]
     memories = [exchange(blocks[j], flips[j]) for j in range(requests)]
     attended = attend(first, memories, served)
 
@@ -301,4 +309,6 @@
         P(),
     )
     out_specs = P("side", ("y", "zl"), ("x", "zh"))
-    return jax.shard_map(body, mesh=torus, in_specs=in_specs, out_specs=out_specs, check_vma=False)
+    return jax.shard_map(
+        body, mesh=torus, in_specs=in_specs, out_specs=out_specs, check_vma=False
+    )

time: 233 us -> 228 us (0.979)
  between operations: 9.53 us -> 3.89 us
where the time goes in v2:
time: 228 us; the launch traced here: 227 us
  waiting for transfers between devices  137 us (60%)
  starting transfers between devices  42.7 us (19%)
  Pallas kernels  24.7 us (11%)
  local copies, waits for them, and re-layouts  15.7 us (7%)
  between operations  3.89 us (2%)
  other arithmetic  3.66 us (2%)
    ppermute x3, waiting for transfers between devices, route(): return lambda b: lax.ppermute(b, ('side', 'y', 'zl'), pairs)  39.5 us
    ppermute x22, waiting for transfers between devices, ring(): lax.ppermute(value, axis, [(i, (i + by) % count) for i in range(count)])  37.2 us
    ppermute x3, waiting for transfers between devices, ring_swap(): return lax.ppermute(value, 'zl', [(i, i ^ bit) for i in range(4)])  28.7 us
    pallas_call x5, Pallas kernels, call(): pl.pallas_call(kernel, out_shape=outs, in_specs=[pl.BlockSpec(memory_spac...  24.7 us
    ppermute x22, starting transfers between devices, ring(): lax.ppermute(value, axis, [(i, (i + by) % count) for i in range(count)])  17.4 us
    ppermute x3, waiting for transfers between devices, body(): got.append(lax.ppermute(part, ('side', 'x'), pairs))  14 us
    ppermute x1, waiting for transfers between devices, body(): taken = lax.ppermute(give, ('side', 'zh'), [(2, 3), (3, 2)])  11.3 us
    ppermute x3, starting transfers between devices, body(): got.append(lax.ppermute(part, ('side', 'x'), pairs))  9.04 us
  transfers between devices with their start and end apart: 33, of which 16 were waited for; matrix products, arithmetic and copies ran while one was open for 5% of the time, Pallas kernels for 3%

profile of v2, /device:TPU:19, one launch (start us, length us, event | category | flops | bytes accessed | tf_op | source)
XLA Modules:
  0.0 227.4 jit_solution(7133868316570382389)
XLA Ops:
  0.0 6.9 %collective-permute-start.51 = (bf16[48,4096]{1,0:T(8,128)(2,1)}, bf16[48,4096]{1,0:T(8,128)(2,1)}, u32[]{:S(2)}, u32[]{:S(2)}) collective-permute-start(bf16[48,4096]{1,0:T(8,128)(2,1)} %bitcast.26), channel_id=1, source_target_pairs={{0,1},{1,0},{2,3},{3,2},{4,5},{5,4},{6,7},{7,6},{8,9},{9,8},{10,11... | collective-permute-start | bytes 1179656 | tf_op jit(solution)/shard_map/ppermute | solution.py:217
  6.9 1.2 collective-permute-start.64
  9.8 1.2 collective-permute-start.48
  11.1 6.1 %collective-permute-done.51.refs_4_ = bf16[48,4096]{1,0:T(8,128)(2,1)} collective-permute-done((bf16[48,4096]{1,0:T(8,128)(2,1)}, bf16[48,4096]{1,0:T(8,128)(2,1)}, u32[]{:S(2)}, u32[]{:S(2)}) %collective-permute-start.51) | collective-permute-done | bytes 393248 | tf_op jit(solution)/shard_map/ppermute | solution.py:217
  17.4 1.6 collective-permute-done.48.refs_1_
  19.5 28.7 %collective-permute-done.64.refs_0_.refs_10_ = bf16[256,1024]{1,0:T(8,128)(2,1)S(1)} collective-permute-done((bf16[256,1024]{1,0:T(8,128)(2,1)}, bf16[256,1024]{1,0:T(8,128)(2,1)S(1)}, u32[]{:S(2)}, u32[]{:S(2)}) %collective-permute-start.64) | collective-permute-done | bytes 524320 | tf_op jit(solution)/shard_map/ppermute | solution.py:20
  48.2 1.1 collective-permute-start.60
  49.3 1.8 collective-permute-start.50
  51.4 9.5 %collective-permute-done.50.refs_3_ = bf16[48,4096]{1,0:T(8,128)(2,1)S(1)} collective-permute-done((bf16[48,4096]{1,0:T(8,128)(2,1)}, bf16[48,4096]{1,0:T(8,128)(2,1)S(1)}, u32[]{:S(2)}, u32[]{:S(2)}) %collective-permute-start.50) | collective-permute-done | bytes 393248 | tf_op jit(solution)/shard_map/ppermute | solution.py:16
  61.3 1.0 collective-permute-start.65
  62.3 4.5 %collective-permute-done.57.refs_11_.refs_3_ = bf16[128,1024]{1,0:T(8,128)(2,1)S(1)} collective-permute-done((bf16[128,1024]{1,0:T(8,128)(2,1)S(1)}, bf16[128,1024]{1,0:T(8,128)(2,1)S(1)}, u32[]{:S(2)}, u32[]{:S(2)}) %collective-permute-start.57) | collective-permute-done | bytes 262176 | tf_op jit(solution)/shard_map/ppermute | solution.py:16
  67.0 1.4 collective-permute-start.70
  68.7 3.9 %collective-permute-done.61.refs_15_.refs_7_ = bf16[256,1024]{1,0:T(8,128)(2,1)S(1)} collective-permute-done((bf16[256,1024]{1,0:T(8,128)(2,1)S(1)}, bf16[256,1024]{1,0:T(8,128)(2,1)S(1)}, u32[]{:S(2)}, u32[]{:S(2)}) %collective-permute-start.61) | collective-permute-done | bytes 524320 | tf_op jit(solution)/shard_map/ppermute | solution.py:16
  72.7 1.2 collective-permute-start.52
  73.9 4.2 %collective-permute-done.65.refs_1_.refs_11_ = bf16[256,1024]{1,0:T(8,128)(2,1)S(1)} collective-permute-done((bf16[256,1024]{1,0:T(8,128)(2,1)S(1)}, bf16[256,1024]{1,0:T(8,128)(2,1)S(1)}, u32[]{:S(2)}, u32[]{:S(2)}) %collective-permute-start.65) | collective-permute-done | bytes 524320 | tf_op jit(solution)/shard_map/ppermute | solution.py:16
  78.3 5.7 %collective-permute-done.66.refs_2_.refs_12_ = bf16[256,1024]{1,0:T(8,128)(2,1)S(1)} collective-permute-done((bf16[256,1024]{1,0:T(8,128)(2,1)S(1)}, bf16[256,1024]{1,0:T(8,128)(2,1)S(1)}, u32[]{:S(2)}, u32[]{:S(2)}) %collective-permute-start.66) | collective-permute-done | bytes 524320 | tf_op jit(solution)/shard_map/ppermute | solution.py:16
  84.0 1.8 collective-permute-start.54
  87.3 2.1 collective-permute-done.70.refs_6_.refs_16_
  89.6 5.6 %collective-permute-done.71.refs_7_.refs_17_ = bf16[256,1024]{1,0:T(8,128)(2,1)S(1)} collective-permute-done((bf16[256,1024]{1,0:T(8,128)(2,1)S(1)}, bf16[256,1024]{1,0:T(8,128)(2,1)S(1)}, u32[]{:S(2)}, u32[]{:S(2)}) %collective-permute-start.71) | collective-permute-done | bytes 524320 | tf_op jit(solution)/shard_map/ppermute | solution.py:16
  95.2 1.6 collective-permute-start.62
  100.2 1.7 slice.73
  104.8 1.5 collective-permute-start.67
  106.3 1.4 collective-permute-start.72
  107.8 1.9 pad_add_fusion.1.lengths_ref
  113.5 7.8 %shard_map.46 = (bf16[384,4096]{1,0:T(8,128)(2,1)}, f32[384,1024]{1,0:T(8,128)}) custom-call(s32[4]{0:T(128)} %pad_add_fusion.pos_ref, bf16[48,4096]{1,0:T(8,128)(2,1)} %bitcast.30, bf16[48,4096]{1,0:T(8,128)(2,1)} %copy-done.22, bf16[48,4096]{1,0:T(8,128)(2,1)} %copy-done.23, bf16[48,4096]{1,0:T(8,128)(2,1)} %copy-done.24, ...), custom_call_target="tpu_custom_call" | custom-call | tf_op jit(solution)/shard_map/pallas_call | solution.py:150
  121.4 6.7 %shard_map.47 = bf16[384,1024]{1,0:T(8,128)(2,1)} custom-call(s32[4]{0:T(128)S(1)} %copy-done.7, bf16[384,4096]{1,0:T(8,128)(2,1)} %get-tuple-element.112.rows_ref, f32[384,1024]{1,0:T(8,128)} %get-tuple-element.113.sum_ref, bf16[256,1024]{1,0:T(8,128)(2,1)S(1)} %collective-permute-done.64.refs_0_.refs_10_, bf16[256,1024]{1,0:T(8,128)(2,1)} %copy-done.10, ...), custom_call_target="tpu_custom_call" | custom-call | tf_op jit(solution)/shard_map/pallas_call | solution.py:150
  128.1 1.0 slice.78.queries_ref
  129.1 3.7 %pad_dynamic-slice_fusion = (bf16[192,1024]{1,0:T(8,128)(2,1)S(1)}, bf16[192,1024]{1,0:T(8,128)(2,1)S(1)}, bf16[192,1024]{1,0:T(8,128)(2,1)S(1)}) fusion(s32[]{:T(128)} %bitcast.15, bf16[384,1024]{1,0:T(8,128)(2,1)} %shard_map.47, s32[]{:T(128)} %bitcast.14, s32[]{:T(128)} %bitcast.13), kind=kLoop, calls=%fused_computation | loop fusion | bytes 1966092 | tf_op jit(solution)/shard_map/dynamic_slice | solution.py:265
  132.8 16.1 %conditional.3 = (bf16[192,1024]{1,0:T(8,128)(2,1)}) conditional(s32[]{:T(128)} %clamp.9, bf16[192,1024]{1,0:T(8,128)(2,1)S(1)} %get-tuple-element.122, bf16[192,1024]{1,0:T(8,128)(2,1)S(1)} %get-tuple-element.122, bf16[192,1024]{1,0:T(8,128)(2,1)S(1)} %get-tuple-element.122, ...), branch_computations={%region_1.2_spmd, %region_2.3_spmd, %region_3.4_spmd, %region_4.5_... | conditional | bytes 1572912 | solution.py:30
  132.9 1.3 collective-permute-start.15
  134.2 14.7 %collective-permute-done.15 = bf16[192,1024]{1,0:T(8,128)(2,1)} collective-permute-done((bf16[192,1024]{1,0:T(8,128)(2,1)S(1)}, bf16[192,1024]{1,0:T(8,128)(2,1)}, u32[]{:S(2)}, u32[]{:S(2)}) %collective-permute-start.15) | collective-permute-done | bytes 393248 | tf_op jit(solution)/shard_map/cond/branch_15_fun/ppermute | solution.py:28
  148.9 10.7 %conditional.4 = (bf16[192,1024]{1,0:T(8,128)(2,1)}) conditional(s32[]{:T(128)} %clamp.10, bf16[192,1024]{1,0:T(8,128)(2,1)S(1)} %get-tuple-element.121, bf16[192,1024]{1,0:T(8,128)(2,1)S(1)} %get-tuple-element.121, bf16[192,1024]{1,0:T(8,128)(2,1)S(1)} %get-tuple-element.121, ...), branch_computations={%region_17.18_spmd, %region_18.19_spmd, %region_19.20_spmd, %regio... | conditional | bytes 1572912 | solution.py:30
  148.9 1.3 collective-permute-start.24
  150.2 9.4 %collective-permute-done.24 = bf16[192,1024]{1,0:T(8,128)(2,1)} collective-permute-done((bf16[192,1024]{1,0:T(8,128)(2,1)S(1)}, bf16[192,1024]{1,0:T(8,128)(2,1)}, u32[]{:S(2)}, u32[]{:S(2)}) %collective-permute-start.24) | collective-permute-done | bytes 393248 | tf_op jit(solution)/shard_map/cond/branch_8_fun/ppermute | solution.py:28
  159.6 16.6 %conditional.5 = (bf16[192,1024]{1,0:T(8,128)(2,1)}) conditional(s32[]{:T(128)} %clamp.11, bf16[192,1024]{1,0:T(8,128)(2,1)S(1)} %get-tuple-element.120, bf16[192,1024]{1,0:T(8,128)(2,1)S(1)} %get-tuple-element.120, bf16[192,1024]{1,0:T(8,128)(2,1)S(1)} %get-tuple-element.120, ...), branch_computations={%region_33.34_spmd, %region_34.35_spmd, %region_35.36_spmd, %regio... | conditional | bytes 1572912 | solution.py:30
  159.6 1.3 collective-permute-start.46
  160.9 15.3 %collective-permute-done.46 = bf16[192,1024]{1,0:T(8,128)(2,1)} collective-permute-done((bf16[192,1024]{1,0:T(8,128)(2,1)S(1)}, bf16[192,1024]{1,0:T(8,128)(2,1)}, u32[]{:S(2)}, u32[]{:S(2)}) %collective-permute-start.46) | collective-permute-done | bytes 393248 | tf_op jit(solution)/shard_map/cond/branch_14_fun/ppermute | solution.py:28
  176.2 2.7 %shard_map.48.attended_ref = bf16[384,512]{1,0:T(8,128)(2,1)S(1)} custom-call(s32[3]{0:T(128)S(1)} %pad_add_fusion.1.lengths_ref, bf16[384,512]{1,0:T(8,128)(2,1)S(1)} %slice.78.queries_ref, bf16[192,1024]{1,0:T(8,128)(2,1)} %get-tuple-element.132.refs_0_, bf16[192,1024]{1,0:T(8,128)(2,1)} %get-tuple-element.133.refs_1_, ...), custom_call_target="tpu_custom_call" | custom-call | tf_op jit(solution)/shard_map/pallas_call | solution.py:150
  179.7 6.0 %shard_map.49 = (bf16[384,1024]{1,0:T(8,128)(2,1)}, bf16[384,1024]{1,0:T(8,128)(2,1)}, bf16[384,1024]{1,0:T(8,128)(2,1)}, f32[384,1024]{1,0:T(8,128)}) custom-call(s32[4]{0:T(128)} %pad_add_fusion.pos_ref, bf16[384,512]{1,0:T(8,128)(2,1)} %copy-done.1, bf16[256,1024]{1,0:T(8,128)(2,1)} %bitcast.25, bf16[256,1024]{1,0:T(8,128)(2,1)} %copy-done.14, ...), custom_call_target="tpu_custom_call" | custom-call | tf_op jit(solution)/shard_map/pallas_call | solution.py:150
  185.7 3.8 %collective-permute-start.74 = (bf16[384,1024]{1,0:T(8,128)(2,1)}, bf16[384,1024]{1,0:T(8,128)(2,1)S(1)}, u32[]{:S(2)}, u32[]{:S(2)}) collective-permute-start(bf16[384,1024]{1,0:T(8,128)(2,1)} %get-tuple-element.115), channel_id=1, source_target_pairs={{128,132},{130,134},{132,128},{134,130},{129,133},{131,135},{133,1... | collective-permute-start | bytes 2359304 | tf_op jit(solution)/shard_map/ppermute | solution.py:285
  189.5 1.9 collective-permute-start.75
  191.4 3.4 %collective-permute-start.76 = (bf16[384,1024]{1,0:T(8,128)(2,1)}, bf16[384,1024]{1,0:T(8,128)(2,1)S(1)}, u32[]{:S(2)}, u32[]{:S(2)}) collective-permute-start(bf16[384,1024]{1,0:T(8,128)(2,1)} %get-tuple-element.117), channel_id=1, source_target_pairs={{128,134},{130,128},{132,130},{134,132},{129,135},{131,129},{133,1... | collective-permute-start | bytes 2359304 | tf_op jit(solution)/shard_map/ppermute | solution.py:285
  194.8 5.5 %collective-permute-done.74.refs_0_ = bf16[384,1024]{1,0:T(8,128)(2,1)S(1)} collective-permute-done((bf16[384,1024]{1,0:T(8,128)(2,1)}, bf16[384,1024]{1,0:T(8,128)(2,1)S(1)}, u32[]{:S(2)}, u32[]{:S(2)}) %collective-permute-start.74) | collective-permute-done | bytes 786464 | tf_op jit(solution)/shard_map/ppermute | solution.py:285
  200.2 8.5 %collective-permute-done.75.refs_1_ = bf16[384,1024]{1,0:T(8,128)(2,1)S(1)} collective-permute-done((bf16[384,1024]{1,0:T(8,128)(2,1)}, bf16[384,1024]{1,0:T(8,128)(2,1)S(1)}, u32[]{:S(2)}, u32[]{:S(2)}) %collective-permute-start.75) | collective-permute-done | bytes 786464 | tf_op jit(solution)/shard_map/ppermute | solution.py:285
  208.7 1.4 copy-done.2
  210.2 1.5 shard_map.50
  211.7 3.5 %collective-permute-start.77 = (bf16[384,512]{1,0:T(8,128)(2,1)S(1)}, bf16[384,512]{1,0:T(8,128)(2,1)S(1)}, u32[]{:S(2)}, u32[]{:S(2)}) collective-permute-start(bf16[384,512]{1,0:T(8,128)(2,1)S(1)} %get-tuple-element.119), channel_id=1, source_target_pairs={{128,129},{129,128},{130,131},{131,130},{132,133},{133,132},{134,1... | collective-permute-start | bytes 1179656 | tf_op jit(solution)/shard_map/ppermute | solution.py:298
  215.2 11.3 %collective-permute-done.77 = bf16[384,512]{1,0:T(8,128)(2,1)S(1)} collective-permute-done((bf16[384,512]{1,0:T(8,128)(2,1)S(1)}, bf16[384,512]{1,0:T(8,128)(2,1)S(1)}, u32[]{:S(2)}, u32[]{:S(2)}) %collective-permute-start.77) | collective-permute-done | bytes 393248 | tf_op jit(solution)/shard_map/ppermute | solution.py:298
  (99 shorter events, 13.9 us)
Async XLA Ops:
  0.0 96.8 %copy-start.26 = (s32[16,3]{0,1:T(4,128)S(1)}, s32[16,3]{0,1:T(4,128)}, u32[]{:S(2)}) copy-start(s32[16,3]{0,1:T(4,128)} %param.55) | copy-start | bytes 580
  0.0 97.4 %copy-start.25 = (s32[16,3]{0,1:T(4,128)S(1)}, s32[16,3]{0,1:T(4,128)}, u32[]{:S(2)}) copy-start(s32[16,3]{0,1:T(4,128)} %param.54) | copy-start | bytes 580
  0.0 17.2 %collective-permute-start.51 = (bf16[48,4096]{1,0:T(8,128)(2,1)}, bf16[48,4096]{1,0:T(8,128)(2,1)}, u32[]{:S(2)}, u32[]{:S(2)}) collective-permute-start(bf16[48,4096]{1,0:T(8,128)(2,1)} %bitcast.26), channel_id=1, source_target_pairs={{0,1},{1,0},{2,3},{3,2},{4,5},{5,4},{6,7},{7,6},{8,9},{9,8},{10,11... | collective-permute-start | bytes 1179656 | tf_op jit(solution)/shard_map/ppermute | solution.py:217
  6.9 41.3 %collective-permute-start.64 = (bf16[256,1024]{1,0:T(8,128)(2,1)}, bf16[256,1024]{1,0:T(8,128)(2,1)S(1)}, u32[]{:S(2)}, u32[]{:S(2)}) collective-permute-start(bf16[256,1024]{1,0:T(8,128)(2,1)} %bitcast.20), channel_id=1, source_target_pairs={{0,16},{8,24},{16,0},{24,8},{1,17},{9,25},{17,1},{25,9},{2,18},{10... | collective-permute-start | bytes 1572872 | tf_op jit(solution)/shard_map/ppermute | solution.py:20
  8.1 40.1 %collective-permute-start.59 = (bf16[256,1024]{1,0:T(8,128)(2,1)}, bf16[256,1024]{1,0:T(8,128)(2,1)S(1)}, u32[]{:S(2)}, u32[]{:S(2)}) collective-permute-start(bf16[256,1024]{1,0:T(8,128)(2,1)} %bitcast.21), channel_id=1, source_target_pairs={{0,8},{8,0},{16,24},{24,16},{1,9},{9,1},{17,25},{25,17},{2,10},{10... | collective-permute-start | bytes 1572872 | tf_op jit(solution)/shard_map/ppermute | solution.py:20
  8.8 40.4 %collective-permute-start.55 = (bf16[256,1024]{1,0:T(8,128)(2,1)}, bf16[256,1024]{1,0:T(8,128)(2,1)S(1)}, u32[]{:S(2)}, u32[]{:S(2)}) collective-permute-start(bf16[256,1024]{1,0:T(8,128)(2,1)} %bitcast.22), channel_id=1, source_target_pairs={{0,32},{32,64},{64,96},{96,0},{1,33},{33,65},{65,97},{97,1},{2,34}... | collective-permute-start | bytes 1572872 | tf_op jit(solution)/shard_map/ppermute | solution.py:16
  9.8 9.2 %collective-permute-start.48 = (bf16[48,4096]{1,0:T(8,128)(2,1)}, bf16[48,4096]{1,0:T(8,128)(2,1)S(1)}, u32[]{:S(2)}, u32[]{:S(2)}) collective-permute-start(bf16[48,4096]{1,0:T(8,128)(2,1)} %bitcast.27), channel_id=1, source_target_pairs={{0,2},{2,4},{4,6},{6,0},{1,3},{3,5},{5,7},{7,1},{8,10},{10,12},{12... | collective-permute-start | bytes 1179656 | tf_op jit(solution)/shard_map/ppermute | solution.py:16
  17.2 34.0 %collective-permute-start.49 = (bf16[48,4096]{1,0:T(8,128)(2,1)}, bf16[48,4096]{1,0:T(8,128)(2,1)S(1)}, u32[]{:S(2)}, u32[]{:S(2)}) collective-permute-start(bf16[48,4096]{1,0:T(8,128)(2,1)} %bitcast.28), channel_id=1, source_target_pairs={{0,6},{2,0},{4,2},{6,4},{1,7},{3,1},{5,3},{7,5},{8,14},{10,8},{12,... | collective-permute-start | bytes 1179656 | tf_op jit(solution)/shard_map/ppermute | solution.py:16
  19.0 32.1 %copy-start.22 = (bf16[48,4096]{1,0:T(8,128)(2,1)}, bf16[48,4096]{1,0:T(8,128)(2,1)S(1)}, u32[]{:S(2)}) copy-start(bf16[48,4096]{1,0:T(8,128)(2,1)S(1)} %collective-permute-done.48.refs_1_) | copy-start | bytes 1179652
  19.0 42.3 %collective-permute-start.56 = (bf16[256,1024]{1,0:T(8,128)(2,1)}, bf16[256,1024]{1,0:T(8,128)(2,1)S(1)}, u32[]{:S(2)}, u32[]{:S(2)}) collective-permute-start(bf16[256,1024]{1,0:T(8,128)(2,1)} %bitcast.23), channel_id=1, source_target_pairs={{0,96},{32,0},{64,32},{96,64},{1,97},{33,1},{65,33},{97,65},{2,98}... | collective-permute-start | bytes 1572872 | tf_op jit(solution)/shard_map/ppermute | solution.py:16
  48.2 73.2 %copy-start = (bf16[256,1024]{1,0:T(8,128)(2,1)}, bf16[256,1024]{1,0:T(8,128)(2,1)S(1)}, u32[]{:S(2)}) copy-start(bf16[256,1024]{1,0:T(8,128)(2,1)S(1)} %collective-permute-done.64.refs_0_.refs_10_) | copy-start | bytes 1572868
  48.2 18.8 %collective-permute-start.69 = (bf16[256,1024]{1,0:T(8,128)(2,1)S(1)}, bf16[256,1024]{1,0:T(8,128)(2,1)S(1)}, u32[]{:S(2)}, u32[]{:S(2)}) collective-permute-start(bf16[256,1024]{1,0:T(8,128)(2,1)S(1)} %collective-permute-done.64.refs_0_.refs_10_), channel_id=1, source_target_pairs={{0,8},{8,0},{16,24},{24,16},{1,9},{9,1},{17,25},{25,17},{2,10},{10... | collective-permute-start | bytes 1572872 | tf_op jit(solution)/shard_map/ppermute | solution.py:20
  48.2 49.1 %copy-start.19 = (bf16[256,1024]{1,0:T(8,128)(2,1)}, bf16[256,1024]{1,0:T(8,128)(2,1)S(1)}, u32[]{:S(2)}) copy-start(bf16[256,1024]{1,0:T(8,128)(2,1)S(1)} %collective-permute-done.59.refs_13_.refs_5_) | copy-start | bytes 1572868
  48.2 20.2 %collective-permute-start.60 = (bf16[256,1024]{1,0:T(8,128)(2,1)S(1)}, bf16[256,1024]{1,0:T(8,128)(2,1)S(1)}, u32[]{:S(2)}, u32[]{:S(2)}) collective-permute-start(bf16[256,1024]{1,0:T(8,128)(2,1)S(1)} %collective-permute-done.59.refs_13_.refs_5_), channel_id=1, source_target_pairs={{0,32},{32,64},{64,96},{96,0},{1,33},{33,65},{65,97},{97,1},{2,34}... | collective-permute-start | bytes 1572872 | tf_op jit(solution)/shard_map/ppermute | solution.py:16
  49.3 45.9 %copy-start.14 = (bf16[256,1024]{1,0:T(8,128)(2,1)}, bf16[256,1024]{1,0:T(8,128)(2,1)S(1)}, u32[]{:S(2)}) copy-start(bf16[256,1024]{1,0:T(8,128)(2,1)S(1)} %collective-permute-done.55.refs_9_.refs_1_) | copy-start | bytes 1572868
  49.3 11.6 %collective-permute-start.50 = (bf16[48,4096]{1,0:T(8,128)(2,1)}, bf16[48,4096]{1,0:T(8,128)(2,1)S(1)}, u32[]{:S(2)}, u32[]{:S(2)}) collective-permute-start(bf16[48,4096]{1,0:T(8,128)(2,1)} %bitcast.29), channel_id=1, source_target_pairs={{0,4},{2,6},{4,0},{6,2},{1,5},{3,7},{5,1},{7,3},{8,12},{10,14},{12... | collective-permute-start | bytes 1179656 | tf_op jit(solution)/shard_map/ppermute | solution.py:16
  51.2 15.6 %collective-permute-start.57 = (bf16[128,1024]{1,0:T(8,128)(2,1)S(1)}, bf16[128,1024]{1,0:T(8,128)(2,1)S(1)}, u32[]{:S(2)}, u32[]{:S(2)}) collective-permute-start(bf16[128,1024]{1,0:T(8,128)(2,1)S(1)} %slice.70), channel_id=1, source_target_pairs={{0,32},{32,64},{64,96},{96,0},{1,33},{33,65},{65,97},{97,1},{2,34}... | collective-permute-start | bytes 786440 | tf_op jit(solution)/shard_map/ppermute | solution.py:16
  60.9 36.5 %copy-start.24 = (bf16[48,4096]{1,0:T(8,128)(2,1)}, bf16[48,4096]{1,0:T(8,128)(2,1)S(1)}, u32[]{:S(2)}) copy-start(bf16[48,4096]{1,0:T(8,128)(2,1)S(1)} %collective-permute-done.50.refs_3_) | copy-start | bytes 1179652
  60.9 11.8 %collective-permute-start.61 = (bf16[256,1024]{1,0:T(8,128)(2,1)S(1)}, bf16[256,1024]{1,0:T(8,128)(2,1)S(1)}, u32[]{:S(2)}, u32[]{:S(2)}) collective-permute-start(bf16[256,1024]{1,0:T(8,128)(2,1)S(1)} %collective-permute-done.59.refs_13_.refs_5_), channel_id=1, source_target_pairs={{0,96},{32,0},{64,32},{96,64},{1,97},{33,1},{65,33},{97,65},{2,98}... | collective-permute-start | bytes 1572872 | tf_op jit(solution)/shard_map/ppermute | solution.py:16
  61.3 42.7 %copy-start.15 = (bf16[256,1024]{1,0:T(8,128)(2,1)}, bf16[256,1024]{1,0:T(8,128)(2,1)S(1)}, u32[]{:S(2)}) copy-start(bf16[256,1024]{1,0:T(8,128)(2,1)S(1)} %collective-permute-done.56.refs_10_.refs_2_) | copy-start | bytes 1572868
  61.3 16.7 %collective-permute-start.65 = (bf16[256,1024]{1,0:T(8,128)(2,1)S(1)}, bf16[256,1024]{1,0:T(8,128)(2,1)S(1)}, u32[]{:S(2)}, u32[]{:S(2)}) collective-permute-start(bf16[256,1024]{1,0:T(8,128)(2,1)S(1)} %collective-permute-done.64.refs_0_.refs_10_), channel_id=1, source_target_pairs={{0,32},{32,64},{64,96},{96,0},{1,33},{33,65},{65,97},{97,1},{2,34}... | collective-permute-start | bytes 1572872 | tf_op jit(solution)/shard_map/ppermute | solution.py:16
  66.8 45.9 %copy-start.20 = (bf16[128,1024]{1,0:T(8,128)(2,1)}, bf16[128,1024]{1,0:T(8,128)(2,1)S(1)}, u32[]{:S(2)}) copy-start(bf16[128,1024]{1,0:T(8,128)(2,1)S(1)} %collective-permute-done.57.refs_11_.refs_3_) | copy-start | bytes 786436
  66.8 17.2 %collective-permute-start.66 = (bf16[256,1024]{1,0:T(8,128)(2,1)S(1)}, bf16[256,1024]{1,0:T(8,128)(2,1)S(1)}, u32[]{:S(2)}, u32[]{:S(2)}) collective-permute-start(bf16[256,1024]{1,0:T(8,128)(2,1)S(1)} %collective-permute-done.64.refs_0_.refs_10_), channel_id=1, source_target_pairs={{0,96},{32,0},{64,32},{96,64},{1,97},{33,1},{65,33},{97,65},{2,98}... | collective-permute-start | bytes 1572872 | tf_op jit(solution)/shard_map/ppermute | solution.py:16
  67.0 30.3 %copy-start.18 = (bf16[256,1024]{1,0:T(8,128)(2,1)}, bf16[256,1024]{1,0:T(8,128)(2,1)S(1)}, u32[]{:S(2)}) copy-start(bf16[256,1024]{1,0:T(8,128)(2,1)S(1)} %collective-permute-done.69.refs_5_.refs_15_) | copy-start | bytes 1572868
  67.0 22.4 %collective-permute-start.70 = (bf16[256,1024]{1,0:T(8,128)(2,1)S(1)}, bf16[256,1024]{1,0:T(8,128)(2,1)S(1)}, u32[]{:S(2)}, u32[]{:S(2)}) collective-permute-start(bf16[256,1024]{1,0:T(8,128)(2,1)S(1)} %collective-permute-done.69.refs_5_.refs_15_), channel_id=1, source_target_pairs={{0,32},{32,64},{64,96},{96,0},{1,33},{33,65},{65,97},{97,1},{2,34}... | collective-permute-start | bytes 1572872 | tf_op jit(solution)/shard_map/ppermute | solution.py:16
  68.4 28.4 %copy-start.16 = (bf16[256,1024]{1,0:T(8,128)(2,1)}, bf16[256,1024]{1,0:T(8,128)(2,1)S(1)}, u32[]{:S(2)}) copy-start(bf16[256,1024]{1,0:T(8,128)(2,1)S(1)} %collective-permute-done.60.refs_14_.refs_6_) | copy-start | bytes 1572868
  68.4 26.8 %collective-permute-start.71 = (bf16[256,1024]{1,0:T(8,128)(2,1)S(1)}, bf16[256,1024]{1,0:T(8,128)(2,1)S(1)}, u32[]{:S(2)}, u32[]{:S(2)}) collective-permute-start(bf16[256,1024]{1,0:T(8,128)(2,1)S(1)} %collective-permute-done.69.refs_5_.refs_15_), channel_id=1, source_target_pairs={{0,96},{32,0},{64,32},{96,64},{1,97},{33,1},{65,33},{97,65},{2,98}... | collective-permute-start | bytes 1572872 | tf_op jit(solution)/shard_map/ppermute | solution.py:16
  72.7 32.1 %collective-permute-start.52 = (bf16[48,4096]{1,0:T(8,128)(2,1)}, bf16[48,4096]{1,0:T(8,128)(2,1)}, u32[]{:S(2)}, u32[]{:S(2)}) collective-permute-start(bf16[48,4096]{1,0:T(8,128)(2,1)} %collective-permute-done.51.refs_4_), channel_id=1, source_target_pairs={{0,2},{2,4},{4,6},{6,0},{1,3},{3,5},{5,7},{7,1},{8,10},{10,12},{12... | collective-permute-start | bytes 1179656 | tf_op jit(solution)/shard_map/ppermute | solution.py:16
  78.1 26.0 %copy-start.10 = (bf16[256,1024]{1,0:T(8,128)(2,1)}, bf16[256,1024]{1,0:T(8,128)(2,1)S(1)}, u32[]{:S(2)}) copy-start(bf16[256,1024]{1,0:T(8,128)(2,1)S(1)} %collective-permute-done.65.refs_1_.refs_11_) | copy-start | bytes 1572868
  78.1 28.2 %collective-permute-start.53 = (bf16[48,4096]{1,0:T(8,128)(2,1)}, bf16[48,4096]{1,0:T(8,128)(2,1)}, u32[]{:S(2)}, u32[]{:S(2)}) collective-permute-start(bf16[48,4096]{1,0:T(8,128)(2,1)} %collective-permute-done.51.refs_4_), channel_id=1, source_target_pairs={{0,6},{2,0},{4,2},{6,4},{1,7},{3,1},{5,3},{7,5},{8,14},{10,8},{12,... | collective-permute-start | bytes 1179656 | tf_op jit(solution)/shard_map/ppermute | solution.py:16
  84.0 20.0 %copy-start.11 = (bf16[256,1024]{1,0:T(8,128)(2,1)}, bf16[256,1024]{1,0:T(8,128)(2,1)S(1)}, u32[]{:S(2)}) copy-start(bf16[256,1024]{1,0:T(8,128)(2,1)S(1)} %collective-permute-done.66.refs_2_.refs_12_) | copy-start | bytes 1572868
  84.0 22.3 %collective-permute-start.54 = (bf16[48,4096]{1,0:T(8,128)(2,1)}, bf16[48,4096]{1,0:T(8,128)(2,1)}, u32[]{:S(2)}, u32[]{:S(2)}) collective-permute-start(bf16[48,4096]{1,0:T(8,128)(2,1)} %collective-permute-done.51.refs_4_), channel_id=1, source_target_pairs={{0,4},{2,6},{4,0},{6,2},{1,5},{3,7},{5,1},{7,3},{8,12},{10,14},{12... | collective-permute-start | bytes 1179656 | tf_op jit(solution)/shard_map/ppermute | solution.py:16
  89.4 31.9 %copy-start.12 = (bf16[256,1024]{1,0:T(8,128)(2,1)}, bf16[256,1024]{1,0:T(8,128)(2,1)S(1)}, u32[]{:S(2)}) copy-start(bf16[256,1024]{1,0:T(8,128)(2,1)S(1)} %collective-permute-done.70.refs_6_.refs_16_) | copy-start | bytes 1572868
  89.4 15.3 %collective-permute-start.58 = (bf16[128,1024]{1,0:T(8,128)(2,1)}, bf16[128,1024]{1,0:T(8,128)(2,1)}, u32[]{:S(2)}, u32[]{:S(2)}) collective-permute-start(bf16[128,1024]{1,0:T(8,128)(2,1)} %slice.71), channel_id=1, source_target_pairs={{0,96},{32,0},{64,32},{96,64},{1,97},{33,1},{65,33},{97,65},{2,98}... | collective-permute-start | bytes 786440 | tf_op jit(solution)/shard_map/ppermute | solution.py:16
  95.2 12.5 %collective-permute-start.62 = (bf16[128,1024]{1,0:T(8,128)(2,1)}, bf16[128,1024]{1,0:T(8,128)(2,1)}, u32[]{:S(2)}, u32[]{:S(2)}) collective-permute-start(bf16[128,1024]{1,0:T(8,128)(2,1)} %slice.72), channel_id=1, source_target_pairs={{0,32},{32,64},{64,96},{96,0},{1,33},{33,65},{65,97},{97,1},{2,34}... | collective-permute-start | bytes 786440 | tf_op jit(solution)/shard_map/ppermute | solution.py:16
  104.8 8.0 %collective-permute-start.63 = (bf16[128,1024]{1,0:T(8,128)(2,1)}, bf16[128,1024]{1,0:T(8,128)(2,1)S(1)}, u32[]{:S(2)}, u32[]{:S(2)}) collective-permute-start(bf16[128,1024]{1,0:T(8,128)(2,1)} %slice.73), channel_id=1, source_target_pairs={{0,96},{32,0},{64,32},{96,64},{1,97},{33,1},{65,33},{97,65},{2,98}... | collective-permute-start | bytes 786440 | tf_op jit(solution)/shard_map/ppermute | solution.py:16
  104.8 16.5 %collective-permute-start.67 = (bf16[128,1024]{1,0:T(8,128)(2,1)}, bf16[128,1024]{1,0:T(8,128)(2,1)S(1)}, u32[]{:S(2)}, u32[]{:S(2)}) collective-permute-start(bf16[128,1024]{1,0:T(8,128)(2,1)} %slice.74), channel_id=1, source_target_pairs={{0,32},{32,64},{64,96},{96,0},{1,33},{33,65},{65,97},{97,1},{2,34}... | collective-permute-start | bytes 786440 | tf_op jit(solution)/shard_map/ppermute | solution.py:16
  106.2 15.1 %collective-permute-start.68 = (bf16[128,1024]{1,0:T(8,128)(2,1)}, bf16[128,1024]{1,0:T(8,128)(2,1)S(1)}, u32[]{:S(2)}, u32[]{:S(2)}) collective-permute-start(bf16[128,1024]{1,0:T(8,128)(2,1)} %slice.75), channel_id=1, source_target_pairs={{0,96},{32,0},{64,32},{96,64},{1,97},{33,1},{65,33},{97,65},{2,98}... | collective-permute-start | bytes 786440 | tf_op jit(solution)/shard_map/ppermute | solution.py:16
  106.3 15.0 %collective-permute-start.72 = (bf16[128,1024]{1,0:T(8,128)(2,1)}, bf16[128,1024]{1,0:T(8,128)(2,1)S(1)}, u32[]{:S(2)}, u32[]{:S(2)}) collective-permute-start(bf16[128,1024]{1,0:T(8,128)(2,1)} %slice.76), channel_id=1, source_target_pairs={{0,32},{32,64},{64,96},{96,0},{1,33},{33,65},{65,97},{97,1},{2,34}... | collective-permute-start | bytes 786440 | tf_op jit(solution)/shard_map/ppermute | solution.py:16
  107.7 13.7 %collective-permute-start.73 = (bf16[128,1024]{1,0:T(8,128)(2,1)}, bf16[128,1024]{1,0:T(8,128)(2,1)S(1)}, u32[]{:S(2)}, u32[]{:S(2)}) collective-permute-start(bf16[128,1024]{1,0:T(8,128)(2,1)} %slice.77), channel_id=1, source_target_pairs={{0,96},{32,0},{64,32},{96,64},{1,97},{33,1},{65,33},{97,65},{2,98}... | collective-permute-start | bytes 786440 | tf_op jit(solution)/shard_map/ppermute | solution.py:16
  132.9 16.0 %collective-permute-start.15 = (bf16[192,1024]{1,0:T(8,128)(2,1)S(1)}, bf16[192,1024]{1,0:T(8,128)(2,1)}, u32[]{:S(2)}, u32[]{:S(2)}) collective-permute-start(bf16[192,1024]{1,0:T(8,128)(2,1)S(1)} %param.15), channel_id=1, source_target_pairs={{0,248},{8,240},{16,232},{24,224},{32,216},{40,208},{48,200},{56,1... | collective-permute-start | bytes 1179656 | tf_op jit(solution)/shard_map/cond/branch_15_fun/ppermute | solution.py:28
  148.9 10.7 %collective-permute-start.24 = (bf16[192,1024]{1,0:T(8,128)(2,1)S(1)}, bf16[192,1024]{1,0:T(8,128)(2,1)}, u32[]{:S(2)}, u32[]{:S(2)}) collective-permute-start(bf16[192,1024]{1,0:T(8,128)(2,1)S(1)} %param.24), channel_id=1, source_target_pairs={{0,192},{8,200},{16,208},{24,216},{32,224},{40,232},{48,240},{56,2... | collective-permute-start | bytes 1179656 | tf_op jit(solution)/shard_map/cond/branch_8_fun/ppermute | solution.py:28
  159.6 16.6 %collective-permute-start.46 = (bf16[192,1024]{1,0:T(8,128)(2,1)S(1)}, bf16[192,1024]{1,0:T(8,128)(2,1)}, u32[]{:S(2)}, u32[]{:S(2)}) collective-permute-start(bf16[192,1024]{1,0:T(8,128)(2,1)S(1)} %param.46), channel_id=1, source_target_pairs={{0,240},{8,248},{16,224},{24,232},{32,208},{40,216},{48,192},{56,2... | collective-permute-start | bytes 1179656 | tf_op jit(solution)/shard_map/cond/branch_14_fun/ppermute | solution.py:28
  179.7 29.0 %copy-start.8 = (s32[4]{0:T(128)S(1)}, s32[4]{0:T(128)}, u32[]{:S(2)}) copy-start(s32[4]{0:T(128)} %pad_add_fusion.pos_ref) | copy-start | bytes 52
  185.7 14.5 %collective-permute-start.74 = (bf16[384,1024]{1,0:T(8,128)(2,1)}, bf16[384,1024]{1,0:T(8,128)(2,1)S(1)}, u32[]{:S(2)}, u32[]{:S(2)}) collective-permute-start(bf16[384,1024]{1,0:T(8,128)(2,1)} %get-tuple-element.115), channel_id=1, source_target_pairs={{128,132},{130,134},{132,128},{134,130},{129,133},{131,135},{133,1... | collective-permute-start | bytes 2359304 | tf_op jit(solution)/shard_map/ppermute | solution.py:285
  189.5 19.3 %collective-permute-start.75 = (bf16[384,1024]{1,0:T(8,128)(2,1)}, bf16[384,1024]{1,0:T(8,128)(2,1)S(1)}, u32[]{:S(2)}, u32[]{:S(2)}) collective-permute-start(bf16[384,1024]{1,0:T(8,128)(2,1)} %get-tuple-element.116), channel_id=1, source_target_pairs={{128,130},{130,132},{132,134},{134,128},{129,131},{131,133},{133,1... | collective-permute-start | bytes 2359304 | tf_op jit(solution)/shard_map/ppermute | solution.py:285
  191.4 17.3 %collective-permute-start.76 = (bf16[384,1024]{1,0:T(8,128)(2,1)}, bf16[384,1024]{1,0:T(8,128)(2,1)S(1)}, u32[]{:S(2)}, u32[]{:S(2)}) collective-permute-start(bf16[384,1024]{1,0:T(8,128)(2,1)} %get-tuple-element.117), channel_id=1, source_target_pairs={{128,134},{130,128},{132,130},{134,132},{129,135},{131,129},{133,1... | collective-permute-start | bytes 2359304 | tf_op jit(solution)/shard_map/ppermute | solution.py:285
  211.7 14.8 %collective-permute-start.77 = (bf16[384,512]{1,0:T(8,128)(2,1)S(1)}, bf16[384,512]{1,0:T(8,128)(2,1)S(1)}, u32[]{:S(2)}, u32[]{:S(2)}) collective-permute-start(bf16[384,512]{1,0:T(8,128)(2,1)S(1)} %get-tuple-element.119), channel_id=1, source_target_pairs={{128,129},{129,128},{130,131},{131,130},{132,133},{133,132},{134,1... | collective-permute-start | bytes 1179656 | tf_op jit(solution)/shard_map/ppermute | solution.py:298
  (12 other events, 91.5 us)
